TPU v7x, 32 devices: a whole 2x2x4 slice. The times are simulated.
32 devices in a mesh: rows: 8 (over z, x), leaf: 4 (over y, core).
Axes of the slice: x: 2, y: 2, z: 4, core: 2. Of those that a mesh axis runs over, the one named last changes fastest.
Arguments:
- right_sides: float32 [65536, 128], P(('rows', 'leaf')), may hold values from -30 to 30
- near_blocks: bfloat16 [2, 128, 512, 512], P(None, ('rows', 'leaf')), may hold values from -1 to 2.4
- leaf_bases: bfloat16 [2, 128, 2, 512, 128], P(None, ('rows', 'leaf')), may hold values from -1.5 to 1.5
- local_factors: bfloat16 [2, 224, 3, 128, 128], P(None, ('rows', 'leaf')), may hold values from -1.7 to 1.7
- upper_factors: bfloat16 [2, 32, 3, 3, 128, 128], P(None, ('rows', 'leaf')), may hold values from -1.7 to 1.7, as said below
- top_couplings: bfloat16 [2, 2, 128, 128], replicated, may hold values from -0.5 to 0.5
Outputs:
- solution: float32 [65536, 128], P(('rows', 'leaf'))
- residual_norms: float32 [3, 128], replicated
Inputs may be any that keep to these rules, and one draw needn't show every extreme that they name: upper_factors[s, d, h] is the same for all devices d with the same d // 2 ** (h + 1): the factors of the node h + 1 levels above device d's own node.
All inputs are finite; a program needn't handle non-finite values.
Results may differ from a plain program's by a relative error of at most 0.00095.
Values sent between devices are 32-bit elements; how exact they have to be, the bound alone decides.
No kernel may reach another device: no remote copies, remote signals or barrier semaphores. Data moves between devices by JAX's collectives and lax.ppermute only.
A program may use at most 128 MiB of HBM per device.

v0:
```python
import functools

import jax
import jax.numpy as jnp
from jax import lax
from jax.experimental import pallas as pl
from jax.experimental.pallas import tpu as pltpu
from jax.sharding import PartitionSpec as P


STEPS = 3
CROSSING = (1, 0)
BF16 = jnp.bfloat16
F32 = jnp.float32
VMEM_LIMIT = 16 * 2**20
START_LIMIT = 48 * 2**20


def mm(left, right):
    return jnp.dot(left, right, preferred_element_type=F32)


def pieces(value):
    high = value.astype(BF16)
    return high, (value - high.astype(F32)).astype(BF16)


def left_mul(table, value):
    high, low = pieces(value)
    width = value.shape[1]
    both = mm(table[0], jnp.concatenate([high, low], axis=1))
    return both[:, :width] + both[:, width:] + mm(table[1], high)


def right_mul(value, table):
    high, low = pieces(value)
    rows = value.shape[0]
    both = mm(jnp.concatenate([high, low], axis=0), table[0])
    return both[:rows] + both[rows:] + mm(high, table[1])


def exact_left(table, value):
    high, low = pieces(value)
    width = value.shape[1]
    both = mm(table, jnp.concatenate([high, low], axis=1))
    return both[:, :width] + both[:, width:]


def exact_right(value, table):
    high, low = pieces(value)
    rows = value.shape[0]
    both = mm(jnp.concatenate([high, low], axis=0), table)
    return both[:rows] + both[rows:]


def chain_left(member, table, value):
    return exact_left(table, value) if member == 0 else mm(table, value.astype(BF16))


def chain_right(member, value, table):
    return exact_right(value, table) if member == 0 else mm(value.astype(BF16), table)


def table_left(member, table, value):
    return left_mul(table, value) if member == 0 else mm(table[0], value.astype(BF16))


def table_right(member, value, table):
    return right_mul(value, table) if member == 0 else mm(value.astype(BF16), table[0])


def put(member, ref, index, value):
    high = value.astype(BF16)
    ref[(0,) + index] = high
    if member == 0:
        ref[(1,) + index] = (value - high.astype(F32)).astype(BF16)


def call(kernel, outs, args, flops, hbm=False, scratch=()):
    specs = [pl.BlockSpec(memory_space=pltpu.HBM if hbm else pltpu.VMEM)] * len(args)
    return pl.pallas_call(
        kernel,
        out_shape=[jax.ShapeDtypeStruct(shape, dtype) for shape, dtype in outs],
        in_specs=specs,
        out_specs=[pl.BlockSpec(memory_space=pltpu.VMEM)] * len(outs),
        scratch_shapes=list(scratch),
        compiler_params=pltpu.CompilerParams(vmem_limit_bytes=START_LIMIT if hbm else VMEM_LIMIT),
        cost_estimate=pl.CostEstimate(flops=flops, bytes_accessed=0, transcendentals=0),
    )(*args)


def level_offsets(leaf_count):
    offsets, count, offset = [], leaf_count, 0
    while count >= 1:
        offsets.append(offset)
        offset += count
        count //= 2
    return offsets


def column_half():
    leaf_size = lax.axis_size("leaf")
    device = lax.axis_index("rows") * leaf_size + lax.axis_index("leaf")
    levels_up = (lax.axis_size("rows") * leaf_size).bit_length() - 1
    half = device % 2
    for number, stage in enumerate(stages_of(levels_up)):
        half = half + device // 2 ** stage[crossing_level(number, stage)] % 2
    return half % 2


def crossing_level(number, stage):
    return min(CROSSING[min(number, 1)], len(stage) - 1)


def masks_of(number, stage):
    low = 2 ** stage[0]
    flip = 2 ** stage[crossing_level(number, stage)]
    masks = (low,) if len(stage) == 1 else (low, 2 * low, 3 * low)
    return tuple(mask ^ 1 if mask & flip else mask for mask in masks)


def send_parts(device, lifted, send_ref, keep_ref):
    columns = lifted.shape[1]
    half = columns // 2
    turned = lifted.T
    first = column_half() == 0
    keep_ref[...] = jnp.where(first, turned[:half], turned[half:])
    send_ref[: device.shape[0]] = device
    send_ref[device.shape[0] :] = jnp.where(first, turned[half:], turned[:half])


def start_kernel(leaves, *refs):
    right_hbm, bases_hbm, local_hbm = refs[:3]
    upper_rows_ref, lower_rows_ref, u0_ref, u1_ref, v0_ref, local0_ref, local1_ref = refs[3:10]
    vt_ref, up_ref, coef_ref, send_ref, keep_ref, v1_ref, semaphores = refs[10:]
    rows = right_hbm.shape[0] // leaves
    middle = right_hbm.shape[0] // 2
    copies = [
        pltpu.make_async_copy(source, target, semaphores.at[index])
        for index, (source, target) in enumerate(
            [
                (local_hbm.at[1], local1_ref),
                (bases_hbm.at[1, :, 1], v1_ref),
                (right_hbm.at[:middle], upper_rows_ref),
                (right_hbm.at[middle:], lower_rows_ref),
                (local_hbm.at[0], local0_ref),
                (bases_hbm.at[0, :, 1], v0_ref),
                (bases_hbm.at[1, :, 0], u1_ref),
                (bases_hbm.at[0, :, 0], u0_ref),
            ]
        )
    ]
    for copy in copies:
        copy.start()
    copies[0].wait()
    rank = local1_ref.shape[-1]
    up_table(1, leaves, local1_ref, up_ref)
    copies[1].wait()
    for leaf in range(leaves):
        vt_ref[leaf] = v1_ref[leaf].T
    copies[2].wait()
    copies[3].wait()
    for leaf in range(leaves):
        value = rows_of((upper_rows_ref, lower_rows_ref), leaf, rows).astype(BF16)
        coef_ref[leaf * rank : (leaf + 1) * rank] = mm(vt_ref[leaf], value)
    lifted = mm(up_ref[0], coef_ref[...].astype(BF16))
    send_parts(lifted[:rank], lifted[rank:], send_ref, keep_ref)
    for copy in copies[4:]:
        copy.wait()


def rows_of(refs, leaf, rows):
    held = refs[0].shape[0] // rows
    place = (leaf % held) * rows
    return refs[leaf // held][place : place + rows]


def up_table(member, leaves, local_ref, up_ref):
    rank = local_ref.shape[-1]
    offsets = level_offsets(leaves)
    turned = {}

    def transfer(node):
        if node not in turned:
            turned[node] = local_ref[node, 0].T
        return turned[node]

    for leaf in range(leaves):
        trail = transfer(leaf).astype(F32)
        for depth in range(1, len(offsets)):
            if depth == len(offsets) - 1:
                put(member, up_ref, (slice(0, rank), pl.ds(leaf * rank, rank)), trail)
            trail = chain_left(member, transfer(offsets[depth] + (leaf >> depth)), trail)
        put(member, up_ref, (slice(rank, 2 * rank), pl.ds(leaf * rank, rank)), trail)


def pack_kernel(base, last, upper_ref, *refs):
    near_ref, far_ref, cross_ref = refs[-3:]
    half = cross_ref.shape[0]
    rank = upper_ref.shape[-1]
    value = refs[0][...]
    if len(refs) == 5:
        value = value + refs[1][rank:]
    risen = chain_right(1, value, upper_ref[1, base, 0])
    near_ref[:half] = value
    far_ref[:half] = risen
    cross_ref[...] = risen
    if not last:
        for member in range(2):
            rows = pl.ds(half + member * rank, rank)
            near_ref[rows] = upper_ref[member, base, 0].astype(F32)
            far_ref[rows] = upper_ref[member, base + 1, 0].astype(F32)


def stage_table_kernel(base, half, upper_ref, near_ref, far_ref, out_ref):
    rank = upper_ref.shape[-1]
    for member in range(2):
        rows = pl.ds(half + member * rank, rank)
        here = upper_ref[member, base + 1, 0]
        put(member, out_ref, (member, pl.ds(0, rank)), mm(upper_ref[member, base, 0], here))
        put(member, out_ref, (member, pl.ds(rank, rank)), mm(near_ref[rows].astype(BF16), here))
        put(member, out_ref, (member, pl.ds(2 * rank, rank)), far_ref[rows])


def local_table_kernel(leaves, *refs):
    local_refs, u_refs = refs[0:2], refs[2:4]
    v0_ref, vt1_ref, up1_ref, vt0_ref, up0_ref, wide_ref, down_ref, feed_ref, chip_ref = refs[4:]
    vt_refs, up_refs = (vt0_ref, vt1_ref), (up0_ref, up1_ref)
    rank = up1_ref.shape[-1] // leaves
    offsets = level_offsets(leaves)
    own = offsets[-1]
    up_table(0, leaves, local_refs[0], up0_ref)
    for leaf in range(leaves):
        vt0_ref[leaf] = v0_ref[leaf].T
    for member in (1, 0):
        other = 1 - member
        local_ref = local_refs[member]
        sign = 1.0 if member == 1 else -1.0
        total = None
        turned = {}

        def transfer(node):
            if node not in turned:
                turned[node] = local_ref[node, 0].T
            return turned[node]

        for leaf in range(leaves):
            rows = pl.ds(leaf * rank, rank)
            trail = None
            for depth in range(len(offsets) - 1):
                node = leaf >> depth
                step = local_ref[offsets[depth] + node, 1]
                coupling = local_ref[offsets[depth] + node, 2]
                coupled = (
                    coupling.astype(F32) if trail is None else chain_right(member, trail, coupling)
                )
                for peer in range(leaves):
                    if peer >> depth != node ^ 1:
                        continue
                    entry = coupled
                    for lower in range(depth - 1, -1, -1):
                        entry = chain_right(
                            member, entry, transfer(offsets[lower] + (peer >> lower))
                        )
                    put(member, wide_ref, (member, rows, pl.ds((1 + peer) * rank, rank)), entry)
                trail = step.astype(F32) if trail is None else chain_right(member, trail, step)
            put(
                member,
                wide_ref,
                (member, rows, pl.ds((1 + leaf) * rank, rank)),
                jnp.zeros((rank, rank), F32),
            )
            put(
                member,
                wide_ref,
                (member, rows, pl.ds(0, rank)),
                chain_right(member, trail, local_ref[own, 2]),
            )
            below = chain_right(member, trail, local_ref[own, 1])
            put(member, down_ref, (member, rows), below)
            basis = mm(vt_refs[other][leaf], u_refs[member][leaf])
            feed = (sign * mm(basis.astype(BF16), below.astype(BF16))).astype(BF16)
            feed_ref[member, rows] = feed
            term = mm(up_refs[other][0, :, pl.ds(leaf * rank, rank)], feed)
            total = term if total is None else total + term
        chip_ref[2 * member] = total[:rank]
        chip_ref[2 * member + 1] = total[rank:].T


def far_table_kernel(upper_ref, top_ref, chip_ref, got_ref, far_ref, sibling_ref):
    position = lax.axis_index("rows") // (lax.axis_size("rows") // 2)
    rank = top_ref.shape[-1]
    for member in range(2):
        sibling_ref[member] = got_ref[2 * member].astype(BF16)
        loop = (chip_ref[2 * member + 1] + got_ref[2 * member + 1]).astype(BF16)
        trail = None
        levels = upper_ref.shape[1] + 1
        for level in range(levels):
            if level == levels - 1:
                coupling = jnp.where(position == 0, top_ref[member, 0], top_ref[member, 1])
            else:
                coupling = upper_ref[member, level, 2]
            coupling = coupling.T
            weight = coupling.astype(F32)
            if trail is not None:
                weight = chain_left(member, coupling, trail)
            if level < levels - 1:
                step = upper_ref[member, level, 1].T
                trail = step.astype(F32) if trail is None else chain_left(member, step, trail)
            rows = pl.ds(level * rank, rank)
            put(member, far_ref, (member, rows, slice(0, rank)), chain_right(member, weight, loop))
            put(member, far_ref, (member, rows, slice(rank, 2 * rank)), weight)


def stage_kernel(member, half, lift, upper_ref, table_ref, own_ref, *refs):
    near_ref, far_ref, cross_ref = refs[:3]
    both = far_ref[:half] + cross_ref[:half]
    value = jnp.concatenate([own_ref[:half], near_ref[:half], both], axis=1)
    total = table_right(member, value, (table_ref[0, member], table_ref[1, member]))
    outs = refs[3:]
    if lift is None:
        outs = outs[-1:]
    elif len(outs) > 2:
        outs = outs[-2:]
    outs[0][:half] = total
    if lift is not None:
        outs[1][:half] = chain_right(member, total, upper_ref[member, lift, 0])
    if outs[0].shape[0] > half:
        for ref in outs:
            ref[half:] = refs[3][...] + refs[4][...]


def far_kernel(member, last, plan, half, upper_ref, table_ref, keep_ref, got_ref, *refs):
    rank = table_ref.shape[-1] // 2
    count = sum(plan)
    parts = []
    place = 0
    for size in plan:
        parts.append(refs[place][:half])
        if size == 3:
            parts.append(refs[place + 1][:half] + refs[place + 2][:half])
        place += size
    value = jnp.concatenate(parts, axis=1)
    total = table_right(member, value, (table_ref[0, member], table_ref[1, member]))
    refs[-1][...] = total[:, rank:]
    if last:
        sums = None
        for ref in refs[:count]:
            if ref.shape[0] == half + 8:
                sums = ref[half:] if sums is None else sums + ref[half:]
        refs[count][...] = sums
    else:
        value = keep_ref[...] + got_ref[rank:] + total[:, :rank]
        refs[count][...] = value
        if len(refs) == count + 3:
            refs[count + 1][...] = chain_right(1 - member, value, upper_ref[1 - member, 0, 0])


def far_rows(mine_ref, theirs_ref):
    mine, theirs = mine_ref[...], theirs_ref[...]
    first = column_half() == 0
    return jnp.concatenate(
        [jnp.where(first, mine, theirs), jnp.where(first, theirs, mine)], axis=0
    ).T


def expand(member, base, far):
    if member == 0:
        return exact_left(base, far)
    return mm(base, far.astype(BF16))


def finish_value(other, rows, leaf, base_refs, u_ref, leaf_far):
    rank = u_ref.shape[-1]
    value = rows_of(base_refs, leaf, rows)
    moved = expand(other, u_ref[leaf], leaf_far[leaf * rank : (leaf + 1) * rank])
    return value + moved if other == 1 else value - moved


def local_kernel(member, first, counts, *refs):
    refs = list(refs)
    near_ref, u_ref, wide_ref, coef_ref, got_ref = (refs.pop(0) for _ in range(5))
    base_refs = tuple(refs.pop(0) for _ in range(counts[0]))
    other_refs = tuple(refs.pop(0) for _ in range(counts[1]))
    other = 1 - member
    leaves, rows, rank = u_ref.shape
    if first:
        coef = coef_ref[...]
        sibling = got_ref[:rank]
    else:
        before_ref, down_ref, feed_ref, sibling_ref, mine_ref, theirs_ref = (
            refs.pop(0) for _ in range(6)
        )
        far = far_rows(mine_ref, theirs_ref)
        rounded = far.astype(BF16)
        coef = coef_ref[...] + mm(feed_ref[other], rounded)
        sibling = got_ref[:rank] + mm(sibling_ref[other], rounded)
        leaf_far = table_left(other, (down_ref[0, other], down_ref[1, other]), far)
    table = (wide_ref[0, member], wide_ref[1, member])
    inner = table_left(member, table, jnp.concatenate([sibling, coef], axis=0))
    norm = None
    for leaf in range(leaves):
        part = slice(leaf * rows, (leaf + 1) * rows)
        small = slice(leaf * rank, (leaf + 1) * rank)
        if first:
            value = rows_of(base_refs, leaf, rows)
        else:
            value = finish_value(other, rows, leaf, base_refs, before_ref, leaf_far)
            if other == 1:
                refs[1][part] = value
            else:
                term = jnp.sum(value * value, axis=0, keepdims=True)
                norm = term if norm is None else norm + term
        near = near_ref[member, leaf]
        if member == 0:
            result = exact_left(near, value)
        else:
            result = mm(near, value.astype(BF16))
        result = result + expand(member, u_ref[leaf], inner[small])
        if member == 0:
            result = rows_of(other_refs, leaf, rows) - result
        elif not first:
            result = rows_of(other_refs, leaf, rows) + result
        refs[0][part] = result
    if norm is not None:
        refs[1][...] = norm


def lift_kernel(other, value_ref, vt_ref, up_ref, next_ref, send_ref, keep_ref):
    leaves, rank, rows = vt_ref.shape
    for leaf in range(leaves):
        value = value_ref[leaf * rows : (leaf + 1) * rows]
        small = slice(leaf * rank, (leaf + 1) * rank)
        if other == 0:
            next_ref[small] = exact_left(vt_ref[leaf], value)
        else:
            next_ref[small] = mm(vt_ref[leaf], value.astype(BF16))
    lifted = table_left(other, (up_ref[0], up_ref[1]), next_ref[...])
    send_parts(lifted[:rank], lifted[rank:], send_ref, keep_ref)


def last_value_kernel(base_ref, u_ref, down_ref, mine_ref, theirs_ref, *refs):
    *old_refs, value_ref, norm_ref = refs
    leaves, rows, _ = u_ref.shape
    far = far_rows(mine_ref, theirs_ref)
    leaf_far = left_mul((down_ref[0, 0], down_ref[1, 0]), far)
    norm = None
    for leaf in range(leaves):
        value = finish_value(0, rows, leaf, (base_ref,), u_ref, leaf_far)
        value_ref[leaf * rows : (leaf + 1) * rows] = value.astype(BF16)
        term = jnp.sum(value * value, axis=0, keepdims=True)
        norm = term if norm is None else norm + term
    norm_ref[...] = jnp.zeros_like(norm_ref)
    for index, ref in enumerate(old_refs):
        norm_ref[index : index + 1] = ref[...]
    norm_ref[len(old_refs) : len(old_refs) + 1] = norm


def last_local_kernel(near_ref, u_ref, wide_ref, coef_ref, got_ref, *refs):
    value_ref, other_ref, feed_ref, sibling_ref, mine_ref, theirs_ref, out_ref = refs
    leaves, rows, rank = u_ref.shape
    far = far_rows(mine_ref, theirs_ref)
    rounded = far.astype(BF16)
    coef = coef_ref[...] + mm(feed_ref[0], rounded)
    sibling = got_ref[:rank] + mm(sibling_ref[0], rounded)
    table = (wide_ref[0, 1], wide_ref[1, 1])
    inner = table_left(1, table, jnp.concatenate([sibling, coef], axis=0))
    for leaf in range(leaves):
        part = slice(leaf * rows, (leaf + 1) * rows)
        result = mm(near_ref[1, leaf], value_ref[part])
        result = result + expand(1, u_ref[leaf], inner[leaf * rank : (leaf + 1) * rank])
        out_ref[part] = other_ref[part] + result


def finish_kernel(u_ref, down_ref, base_ref, mine_ref, theirs_ref, out_ref):
    leaves, rows, _ = u_ref.shape
    far = far_rows(mine_ref, theirs_ref)
    leaf_far = table_left(1, (down_ref[0, 1], down_ref[1, 1]), far)
    for leaf in range(leaves):
        value = finish_value(1, rows, leaf, (base_ref,), u_ref, leaf_far)
        out_ref[leaf * rows : (leaf + 1) * rows] = value


def body(right_sides, near_blocks, leaf_bases, local_factors, upper_factors, top_couplings):
    bits_leaf = lax.axis_size("leaf").bit_length() - 1
    bits_rows = lax.axis_size("rows").bit_length() - 1
    devices = lax.axis_size("rows") * lax.axis_size("leaf")
    leaves = near_blocks.shape[1]
    columns = right_sides.shape[1]
    rank = leaf_bases.shape[-1]
    half = columns // 2
    stages = stages_of(bits_leaf + bits_rows)

    def swap(value, mask):
        pairs = [(source, source ^ mask) for source in range(devices)]
        return lax.ppermute(value, ("rows", "leaf"), pairs)

    unit = 2 * rank * rank * columns
    message = ((half, rank), F32)
    lifted = ((rank + half, rank), F32)
    coefs = ((leaves * rank, columns), F32)
    size = (right_sides.shape, F32)
    wide_half = ((right_sides.shape[0] // 2, columns), F32)
    basis = ((leaves, leaf_bases.shape[3], rank), BF16)
    turned = ((leaves, rank, leaf_bases.shape[3]), BF16)
    node = (local_factors.shape[1:], BF16)
    rises = ((2, 2 * rank, leaves * rank), BF16)
    loaded = call(
        functools.partial(start_kernel, leaves),
        [wide_half, wide_half, basis, basis, basis, node, node, turned, rises, coefs, lifted, message],
        [right_sides, leaf_bases, local_factors],
        150 * unit,
        hbm=True,
        scratch=[pltpu.VMEM(*basis), pltpu.SemaphoreType.DMA((8,))],
    )
    right = loaded[:2]
    u = loaded[2:4]
    v_operator, local_operator, local_inverse, vt_inverse, up_inverse = loaded[4:9]
    coef, send, keep = loaded[9:]
    got = swap(send, 1)
    near = near_blocks
    upper = upper_factors[:, 0]

    vt = [None, vt_inverse]
    up = [None, up_inverse]
    stage_tables, plan = [], []
    member = 1
    base = current = right
    chip = chip_risen = None
    norms = []
    mine = theirs = None
    applies = 2 * STEPS + 1
    plan = [1 if len(stage) == 1 else 3 for stage in stages]
    for index in range(applies):
        last = index == applies - 1
        other = 1 - member
        arrived = []
        value, risen = chip, chip_risen
        norm = None
        for number, stage in enumerate(stages):
            lower_level = stage[0] - 1
            top_stage = number == len(stages) - 1
            masks = masks_of(number, stage)
            sent = [value, risen, risen][: len(masks)]
            if index == 0 and len(stage) > 1:
                tall = message if top_stage else ((half + 2 * rank, rank), F32)
                if number == 0 or not top_stage:
                    sent = call(
                        functools.partial(pack_kernel, lower_level, top_stage),
                        [tall, tall, message],
                        [upper] + ([value] if number else [keep, got]),
                        unit,
                    )
                value = sent[0]
            elif index == 0 and value is None:
                value = keep + got[rank:]
                sent = [value] * len(masks)
            batch = [swap(data, mask) for data, mask in zip(sent, masks)]
            arrived += batch
            if index == 0 and not top_stage:
                stage_tables += call(
                    functools.partial(stage_table_kernel, lower_level, half),
                    [((2, 2, 3 * rank, rank), BF16)],
                    [upper] + batch[:2],
                    16 * unit,
                )
            if number == 0:
                if index == 0:
                    tables = call(
                        functools.partial(local_table_kernel, leaves),
                        [
                            turned,
                            rises,
                            ((2, 2, leaves * rank, (leaves + 1) * rank), BF16),
                            ((2, 2, leaves * rank, rank), BF16),
                            ((2, leaves * rank, rank), BF16),
                            ((4, rank, rank), F32),
                        ],
                        [local_operator, local_inverse] + list(u) + [v_operator, vt_inverse, up_inverse],
                        300 * unit,
                    )
                    vt[0], up[0], wide, down, feed, chip_feed = tables
                    chip_got = swap(chip_feed, 1)
                if last:
                    finished, norm = call(
                        last_value_kernel,
                        [(right_sides.shape, BF16), ((8, columns), F32)],
                        [base, u[0], down, mine, theirs] + norms,
                        100 * unit,
                    )
                    norm_got = swap(norm, 1)
                    base = call(
                        last_local_kernel,
                        [size],
                        [near, u[1], wide, coef, got, finished, current, feed, sibling_table]
                        + [mine, theirs],
                        100 * unit,
                    )[0]
                else:
                    args = [near, u[member], wide, coef, got]
                    base_list = list(base) if isinstance(base, (list, tuple)) else [base]
                    other_list = list(right) if member == 0 else [] if index == 0 else [current]
                    args += base_list + other_list
                    if index:
                        args += [u[other], down, feed, sibling_table, mine, theirs]
                    outs = [size]
                    if index:
                        outs.append(size if member == 0 else ((1, columns), F32))
                    counts = (len(base_list), len(other_list))
                    results = call(
                        functools.partial(local_kernel, member, index == 0, counts),
                        outs,
                        args,
                        200 * unit,
                    )
                    base = results[0]
                    coef, send, next_keep = call(
                        functools.partial(lift_kernel, other),
                        [coefs, lifted, message],
                        [base, vt[other], up[other]],
                        100 * unit,
                    )
                    next_got = swap(send, 1)
                    if index and member == 0:
                        current = results[1]
                    elif index:
                        norms.append(results[1])
            if not top_stage:
                extra = [norm, norm_got] if last and number == len(stages) - 2 else []
                shape = ((half + (8 if extra else 0), rank), F32)
                lift = stages[number + 1][0] - 1 if len(stages[number + 1]) > 1 else None
                results = call(
                    functools.partial(stage_kernel, member, half, lift),
                    [shape] * (1 if lift is None else 2),
                    [upper, stage_tables[number], value] + batch + extra,
                    8 * unit,
                )
                value, risen = results[0], results[-1]
        if index == 0:
            far_table, sibling_table = call(
                far_table_kernel,
                [
                    ((2, 2, (upper.shape[1] + 1) * rank, 2 * rank), BF16),
                    ((2, rank, rank), BF16),
                ],
                [upper, top_couplings, chip_feed, chip_got],
                100 * unit,
            )
        outs = [((8, columns), F32), message]
        if not last:
            outs = [message] * (3 if len(stages[0]) > 1 else 2)
        results = call(
            functools.partial(far_kernel, member, last, plan, half),
            outs,
            [upper, far_table] + ([keep, got] if last else [next_keep, next_got]) + arrived,
            20 * unit,
        )
        chip, chip_risen, mine = results[0], results[-2], results[-1]
        theirs = swap(mine, 1)
        if last:
            sums = chip + value[half:]
        else:
            keep, got = next_keep, next_got
        member = other
    solution = call(finish_kernel, [size], [u[1], down, base, mine, theirs], 30 * unit)[0]
    for number, stage in enumerate(stages[:-1]):
        masks = masks_of(number, stage)
        sums = sum([swap(sums, mask) for mask in masks], sums)
    return solution, sums[:STEPS]


def stages_of(levels_up):
    return [tuple(range(level, min(level + 2, levels_up))) for level in range(1, levels_up, 2)]


def solution(mesh):
    placed = (
        P(("rows", "leaf"), None),
        P(None, ("rows", "leaf"), None, None),
        P(None, ("rows", "leaf"), None, None, None),
        P(None, ("rows", "leaf"), None, None, None),
        P(None, ("rows", "leaf"), None, None, None, None),
        P(),
    )

    return jax.shard_map(
        body,
        mesh=mesh,
        in_specs=placed,
        out_specs=(P(("rows", "leaf"), None), P()),
        check_vma=False,
    )
```

profile of v0, /device:TPU:0, one launch (start us, length us, event | category | flops | bytes accessed | tf_op | source)
XLA Modules:
  0.0 142.8 jit_solution(2326508536040719310)
XLA Ops:
  0.6 2.3 %shard_map.77 = (f32[1024,128]{1,0:T(8,128)S(1)}, f32[1024,128]{1,0:T(8,128)S(1)}, bf16[4,512,128]{2,1,0:T(8,128)(2,1)S(1)}, bf16[4,512,128]{2,1,0:T(8,128)(2,1)...) custom-call(f32[2048,128]{1,0:T(8,128)} %refs_0_.7, ...), custom_call_target="tpu_custom_call" | custom-call | flops 629145600 | tf_op jit(solution)/shard_map/pallas_call | solution.py:81
  3.5 4.2 %shard_map.78 = (bf16[4,128,512]{2,1,0:T(8,128)(2,1)S(1)}, bf16[2,256,512]{2,1,0:T(8,128)(2,1)S(1)}, bf16[2,2,512,640]{3,2,1,0:T(8,128)(2,1)S(1)}, bf16[2,2,512,...) custom-call(bf16[7,3,128,128]{3,2,1,0:T(8,128)(2,1)S(1)} %get-tuple-element.90.refs_0_, ...), custom_call_target="tpu_custom_call" | custom-call | flops 1258291200 | tf_op jit(solution)/shard_map/pallas_call | solution.py:81
  8.0 3.0 %collective-permute-start.3 = (f32[320,128]{1,0:T(8,128)S(1)}, f32[320,128]{1,0:T(8,128)S(1)}, u32[]{:S(2)}, u32[]{:S(2)}) collective-permute-start(f32[320,128]{1,0:T(8,128)S(1)} %get-tuple-element.112.own_ref), channel_id=1, source_target_pairs={{0,2},{1,3},{2,0},{3,1},{4,6},{5,7},{6,4},{7,5},{8,10},{9,11},{10,... | collective-permute-start | bytes 491528 | tf_op jit(solution)/shard_map/ppermute | solution.py:496
  15.4 2.1 %collective-permute-done.4.far_ref.refs_1_ = f32[320,128]{1,0:T(8,128)S(1)} collective-permute-done((f32[320,128]{1,0:T(8,128)S(1)}, f32[320,128]{1,0:T(8,128)S(1)}, u32[]{:S(2)}, u32[]{:S(2)}) %collective-permute-start.4) | collective-permute-done | bytes 163872 | tf_op jit(solution)/shard_map/ppermute | solution.py:496
  19.3 2.6 %collective-permute-start.7 = (f32[64,128]{1,0:T(8,128)S(1)}, f32[64,128]{1,0:T(8,128)S(1)}, u32[]{:S(2)}, u32[]{:S(2)}) collective-permute-start(f32[64,128]{1,0:T(8,128)S(1)} %get-tuple-element.116), channel_id=1, source_target_pairs={{0,16},{1,17},{2,18},{3,19},{4,20},{5,21},{6,22},{7,23},{8,24},{9,... | collective-permute-start | bytes 98312 | tf_op jit(solution)/shard_map/ppermute | solution.py:496
  24.0 2.0 %collective-permute-done.6.refs_3_ = f32[64,128]{1,0:T(8,128)S(1)} collective-permute-done((f32[64,128]{1,0:T(8,128)S(1)}, f32[64,128]{1,0:T(8,128)S(1)}, u32[]{:S(2)}, u32[]{:S(2)}) %collective-permute-start.6) | collective-permute-done | bytes 32800 | tf_op jit(solution)/shard_map/ppermute | solution.py:496
  29.0 2.1 %shard_map.86 = (f32[2048,128]{1,0:T(8,128)S(1)}, f32[2048,128]{1,0:T(8,128)S(1)}) custom-call(bf16[2,4,512,512]{3,2,1,0:T(8,128)(2,1)S(1)} %copy-done, bf16[4,512,128]{2,1,0:T(8,128)(2,1)S(1)} %get-tuple-element.92.refs_2_.refs_1_.refs_7_.u_ref, bf16[2,2,512,640]{3,2,1,0:T(8,128)(2,1)S(1)} %get-tuple-element.97.refs_2_.wide_ref, ...), custom_call_target="tpu_custom_call" | custom-call | flops 838860800 | tf_op jit(solution)/shard_map/pallas_call | solution.py:81
  35.8 2.0 %collective-permute-done.13.refs_2_ = f32[64,128]{1,0:T(8,128)S(1)} collective-permute-done((f32[64,128]{1,0:T(8,128)S(1)}, f32[64,128]{1,0:T(8,128)S(1)}, u32[]{:S(2)}, u32[]{:S(2)}) %collective-permute-start.13) | collective-permute-done | bytes 32800 | tf_op jit(solution)/shard_map/ppermute | solution.py:496
  38.4 2.2 %collective-permute-start.15 = (f32[64,128]{1,0:T(8,128)S(1)}, f32[64,128]{1,0:T(8,128)S(1)}, u32[]{:S(2)}, u32[]{:S(2)}) collective-permute-start(f32[64,128]{1,0:T(8,128)S(1)} %get-tuple-element.126), channel_id=1, source_target_pairs={{0,16},{1,17},{2,18},{3,19},{4,20},{5,21},{6,22},{7,23},{8,24},{9,... | collective-permute-start | bytes 98312 | tf_op jit(solution)/shard_map/ppermute | solution.py:496
  43.2 2.9 %collective-permute-done.16.refs_5_ = f32[64,128]{1,0:T(8,128)S(1)} collective-permute-done((f32[64,128]{1,0:T(8,128)S(1)}, f32[64,128]{1,0:T(8,128)S(1)}, u32[]{:S(2)}, u32[]{:S(2)}) %collective-permute-start.16) | collective-permute-done | bytes 32800 | tf_op jit(solution)/shard_map/ppermute | solution.py:496
  47.6 1.9 %shard_map.90 = (f32[2048,128]{1,0:T(8,128)S(1)}, f32[1,128]{1,0:T(1,128)S(1)}) custom-call(bf16[2,4,512,512]{3,2,1,0:T(8,128)(2,1)S(1)} %copy-done, bf16[4,512,128]{2,1,0:T(8,128)(2,1)S(1)} %get-tuple-element.89.refs_3_.refs_1_.refs_8_.u_ref, bf16[2,2,512,640]{3,2,1,0:T(8,128)(2,1)S(1)} %get-tuple-element.97.refs_2_.wide_ref, ...), custom_call_target="tpu_custom_call" | custom-call | flops 838860800 | tf_op jit(solution)/shard_map/pallas_call | solution.py:81
  54.4 2.0 %collective-permute-done.21.refs_2_ = f32[64,128]{1,0:T(8,128)S(1)} collective-permute-done((f32[64,128]{1,0:T(8,128)S(1)}, f32[64,128]{1,0:T(8,128)S(1)}, u32[]{:S(2)}, u32[]{:S(2)}) %collective-permute-start.21) | collective-permute-done | bytes 32800 | tf_op jit(solution)/shard_map/ppermute | solution.py:496
  56.6 2.5 %collective-permute-start.23 = (f32[64,128]{1,0:T(8,128)S(1)}, f32[64,128]{1,0:T(8,128)S(1)}, u32[]{:S(2)}, u32[]{:S(2)}) collective-permute-start(f32[64,128]{1,0:T(8,128)S(1)} %get-tuple-element.135), channel_id=1, source_target_pairs={{0,16},{1,17},{2,18},{3,19},{4,20},{5,21},{6,22},{7,23},{8,24},{9,... | collective-permute-start | bytes 98312 | tf_op jit(solution)/shard_map/ppermute | solution.py:496
  61.5 3.1 %collective-permute-done.24.refs_5_ = f32[64,128]{1,0:T(8,128)S(1)} collective-permute-done((f32[64,128]{1,0:T(8,128)S(1)}, f32[64,128]{1,0:T(8,128)S(1)}, u32[]{:S(2)}, u32[]{:S(2)}) %collective-permute-start.24) | collective-permute-done | bytes 32800 | tf_op jit(solution)/shard_map/ppermute | solution.py:496
  66.1 2.1 %shard_map.94 = (f32[2048,128]{1,0:T(8,128)S(1)}, f32[2048,128]{1,0:T(8,128)S(1)}) custom-call(bf16[2,4,512,512]{3,2,1,0:T(8,128)(2,1)S(1)} %copy-done, bf16[4,512,128]{2,1,0:T(8,128)(2,1)S(1)} %get-tuple-element.92.refs_2_.refs_1_.refs_7_.u_ref, bf16[2,2,512,640]{3,2,1,0:T(8,128)(2,1)S(1)} %get-tuple-element.97.refs_2_.wide_ref, ...), custom_call_target="tpu_custom_call" | custom-call | flops 838860800 | tf_op jit(solution)/shard_map/pallas_call | solution.py:81
  70.8 1.5 %collective-permute-start.29 = (f32[64,128]{1,0:T(8,128)S(1)}, f32[64,128]{1,0:T(8,128)S(1)}, u32[]{:S(2)}, u32[]{:S(2)}) collective-permute-start(f32[64,128]{1,0:T(8,128)S(1)} %get-tuple-element.143), channel_id=1, source_target_pairs={{0,7},{1,6},{2,5},{3,4},{4,3},{5,2},{6,1},{7,0},{8,15},{9,14},{10,... | collective-permute-start | bytes 98312 | tf_op jit(solution)/shard_map/ppermute | solution.py:496
  73.0 2.0 %collective-permute-done.29.refs_2_ = f32[64,128]{1,0:T(8,128)S(1)} collective-permute-done((f32[64,128]{1,0:T(8,128)S(1)}, f32[64,128]{1,0:T(8,128)S(1)}, u32[]{:S(2)}, u32[]{:S(2)}) %collective-permute-start.29) | collective-permute-done | bytes 32800 | tf_op jit(solution)/shard_map/ppermute | solution.py:496
  75.3 2.5 %collective-permute-start.31 = (f32[64,128]{1,0:T(8,128)S(1)}, f32[64,128]{1,0:T(8,128)S(1)}, u32[]{:S(2)}, u32[]{:S(2)}) collective-permute-start(f32[64,128]{1,0:T(8,128)S(1)} %get-tuple-element.145), channel_id=1, source_target_pairs={{0,16},{1,17},{2,18},{3,19},{4,20},{5,21},{6,22},{7,23},{8,24},{9,... | collective-permute-start | bytes 98312 | tf_op jit(solution)/shard_map/ppermute | solution.py:496
  80.2 3.1 %collective-permute-done.32.refs_5_ = f32[64,128]{1,0:T(8,128)S(1)} collective-permute-done((f32[64,128]{1,0:T(8,128)S(1)}, f32[64,128]{1,0:T(8,128)S(1)}, u32[]{:S(2)}, u32[]{:S(2)}) %collective-permute-start.32) | collective-permute-done | bytes 32800 | tf_op jit(solution)/shard_map/ppermute | solution.py:496
  84.8 1.9 %shard_map.98 = (f32[2048,128]{1,0:T(8,128)S(1)}, f32[1,128]{1,0:T(1,128)S(1)}) custom-call(bf16[2,4,512,512]{3,2,1,0:T(8,128)(2,1)S(1)} %copy-done, bf16[4,512,128]{2,1,0:T(8,128)(2,1)S(1)} %get-tuple-element.89.refs_3_.refs_1_.refs_8_.u_ref, bf16[2,2,512,640]{3,2,1,0:T(8,128)(2,1)S(1)} %get-tuple-element.97.refs_2_.wide_ref, ...), custom_call_target="tpu_custom_call" | custom-call | flops 838860800 | tf_op jit(solution)/shard_map/pallas_call | solution.py:81
  91.6 2.0 %collective-permute-done.37.refs_2_ = f32[64,128]{1,0:T(8,128)S(1)} collective-permute-done((f32[64,128]{1,0:T(8,128)S(1)}, f32[64,128]{1,0:T(8,128)S(1)}, u32[]{:S(2)}, u32[]{:S(2)}) %collective-permute-start.37) | collective-permute-done | bytes 32800 | tf_op jit(solution)/shard_map/ppermute | solution.py:496
  93.8 2.5 %collective-permute-start.39 = (f32[64,128]{1,0:T(8,128)S(1)}, f32[64,128]{1,0:T(8,128)S(1)}, u32[]{:S(2)}, u32[]{:S(2)}) collective-permute-start(f32[64,128]{1,0:T(8,128)S(1)} %get-tuple-element.154), channel_id=1, source_target_pairs={{0,16},{1,17},{2,18},{3,19},{4,20},{5,21},{6,22},{7,23},{8,24},{9,... | collective-permute-start | bytes 98312 | tf_op jit(solution)/shard_map/ppermute | solution.py:496
  98.6 3.1 %collective-permute-done.40.refs_5_ = f32[64,128]{1,0:T(8,128)S(1)} collective-permute-done((f32[64,128]{1,0:T(8,128)S(1)}, f32[64,128]{1,0:T(8,128)S(1)}, u32[]{:S(2)}, u32[]{:S(2)}) %collective-permute-start.40) | collective-permute-done | bytes 32800 | tf_op jit(solution)/shard_map/ppermute | solution.py:496
  103.3 2.1 %shard_map.102 = (f32[2048,128]{1,0:T(8,128)S(1)}, f32[2048,128]{1,0:T(8,128)S(1)}) custom-call(bf16[2,4,512,512]{3,2,1,0:T(8,128)(2,1)S(1)} %copy-done, bf16[4,512,128]{2,1,0:T(8,128)(2,1)S(1)} %get-tuple-element.92.refs_2_.refs_1_.refs_7_.u_ref, bf16[2,2,512,640]{3,2,1,0:T(8,128)(2,1)S(1)} %get-tuple-element.97.refs_2_.wide_ref, ...), custom_call_target="tpu_custom_call" | custom-call | flops 838860800 | tf_op jit(solution)/shard_map/pallas_call | solution.py:81
  110.1 2.0 %collective-permute-done.45.refs_2_ = f32[64,128]{1,0:T(8,128)S(1)} collective-permute-done((f32[64,128]{1,0:T(8,128)S(1)}, f32[64,128]{1,0:T(8,128)S(1)}, u32[]{:S(2)}, u32[]{:S(2)}) %collective-permute-start.45) | collective-permute-done | bytes 32800 | tf_op jit(solution)/shard_map/ppermute | solution.py:496
  112.4 2.5 %collective-permute-start.47 = (f32[64,128]{1,0:T(8,128)S(1)}, f32[64,128]{1,0:T(8,128)S(1)}, u32[]{:S(2)}, u32[]{:S(2)}) collective-permute-start(f32[64,128]{1,0:T(8,128)S(1)} %get-tuple-element.163), channel_id=1, source_target_pairs={{0,16},{1,17},{2,18},{3,19},{4,20},{5,21},{6,22},{7,23},{8,24},{9,... | collective-permute-start | bytes 98312 | tf_op jit(solution)/shard_map/ppermute | solution.py:496
  117.3 3.1 %collective-permute-done.48.refs_5_ = f32[64,128]{1,0:T(8,128)S(1)} collective-permute-done((f32[64,128]{1,0:T(8,128)S(1)}, f32[64,128]{1,0:T(8,128)S(1)}, u32[]{:S(2)}, u32[]{:S(2)}) %collective-permute-start.48) | collective-permute-done | bytes 32800 | tf_op jit(solution)/shard_map/ppermute | solution.py:496
  124.9 1.8 %collective-permute-done.50.refs_0_ = f32[64,128]{1,0:T(8,128)S(1)} collective-permute-done((f32[64,128]{1,0:T(8,128)S(1)}, f32[64,128]{1,0:T(8,128)S(1)}, u32[]{:S(2)}, u32[]{:S(2)}) %collective-permute-start.50) | collective-permute-done | bytes 32800 | tf_op jit(solution)/shard_map/ppermute | solution.py:496
  127.0 2.0 %collective-permute-start.55 = (f32[72,128]{1,0:T(8,128)S(1)}, f32[72,128]{1,0:T(8,128)S(1)}, u32[]{:S(2)}, u32[]{:S(2)}) collective-permute-start(f32[72,128]{1,0:T(8,128)S(1)} %get-tuple-element.173), channel_id=1, source_target_pairs={{0,16},{1,17},{2,18},{3,19},{4,20},{5,21},{6,22},{7,23},{8,24},{9,... | collective-permute-start | bytes 110600 | tf_op jit(solution)/shard_map/ppermute | solution.py:496
  129.0 1.9 %collective-permute-start.56 = (f32[72,128]{1,0:T(8,128)S(1)}, f32[72,128]{1,0:T(8,128)S(1)}, u32[]{:S(2)}, u32[]{:S(2)}) collective-permute-start(f32[72,128]{1,0:T(8,128)S(1)} %get-tuple-element.173), channel_id=1, source_target_pairs={{0,25},{1,24},{2,27},{3,26},{4,29},{5,28},{6,31},{7,30},{8,17},{9,... | collective-permute-start | bytes 110600 | tf_op jit(solution)/shard_map/ppermute | solution.py:496
  131.9 2.2 %collective-permute-done.56.refs_5_ = f32[72,128]{1,0:T(8,128)S(1)} collective-permute-done((f32[72,128]{1,0:T(8,128)S(1)}, f32[72,128]{1,0:T(8,128)S(1)}, u32[]{:S(2)}, u32[]{:S(2)}) %collective-permute-start.56) | collective-permute-done | bytes 36896 | tf_op jit(solution)/shard_map/ppermute | solution.py:496
  139.2 1.5 %collective-permute-done.58 = f32[8,128]{1,0:T(8,128)S(1)} collective-permute-done((f32[8,128]{1,0:T(8,128)S(1)}, f32[8,128]{1,0:T(8,128)S(1)}, u32[]{:S(2)}, u32[]{:S(2)}) %collective-permute-start.58) | collective-permute-done | bytes 4128 | tf_op jit(solution)/shard_map/ppermute | solution.py:496
  (133 shorter events, 67.5 us)
Async XLA Ops:
  3.0 4.9 %collective-permute-start = (f32[192,128]{1,0:T(8,128)S(1)}, f32[192,128]{1,0:T(8,128)S(1)}, u32[]{:S(2)}, u32[]{:S(2)}) collective-permute-start(f32[192,128]{1,0:T(8,128)S(1)} %get-tuple-element.99), channel_id=1, source_target_pairs={{0,1},{1,0},{2,3},{3,2},{4,5},{5,4},{6,7},{7,6},{8,9},{9,8},{10,11... | collective-permute-start | bytes 294920 | tf_op jit(solution)/shard_map/ppermute | solution.py:496
  7.8 15.1 %collective-permute-start.2 = (f32[4,128,128]{2,1,0:T(8,128)S(1)}, f32[4,128,128]{2,1,0:T(8,128)S(1)}, u32[]{:S(2)}, u32[]{:S(2)}) collective-permute-start(f32[4,128,128]{2,1,0:T(8,128)S(1)} %get-tuple-element.107.chip_ref), channel_id=1, source_target_pairs={{0,1},{1,0},{2,3},{3,2},{4,5},{5,4},{6,7},{7,6},{8,9},{9,8},{10,11... | collective-permute-start | bytes 786440 | tf_op jit(solution)/shard_map/ppermute | solution.py:496
  8.0 7.4 %collective-permute-start.3 = (f32[320,128]{1,0:T(8,128)S(1)}, f32[320,128]{1,0:T(8,128)S(1)}, u32[]{:S(2)}, u32[]{:S(2)}) collective-permute-start(f32[320,128]{1,0:T(8,128)S(1)} %get-tuple-element.112.own_ref), channel_id=1, source_target_pairs={{0,2},{1,3},{2,0},{3,1},{4,6},{5,7},{6,4},{7,5},{8,10},{9,11},{10,... | collective-permute-start | bytes 491528 | tf_op jit(solution)/shard_map/ppermute | solution.py:496
  11.0 6.5 %collective-permute-start.4 = (f32[320,128]{1,0:T(8,128)S(1)}, f32[320,128]{1,0:T(8,128)S(1)}, u32[]{:S(2)}, u32[]{:S(2)}) collective-permute-start(f32[320,128]{1,0:T(8,128)S(1)} %get-tuple-element.113), channel_id=1, source_target_pairs={{0,5},{1,4},{2,7},{3,6},{4,1},{5,0},{6,3},{7,2},{8,13},{9,12},{10,... | collective-permute-start | bytes 491528 | tf_op jit(solution)/shard_map/ppermute | solution.py:496
  13.9 10.1 %collective-permute-start.1 = (f32[192,128]{1,0:T(8,128)S(1)}, f32[192,128]{1,0:T(8,128)S(1)}, u32[]{:S(2)}, u32[]{:S(2)}) collective-permute-start(f32[192,128]{1,0:T(8,128)S(1)} %get-tuple-element.105), channel_id=1, source_target_pairs={{0,1},{1,0},{2,3},{3,2},{4,5},{5,4},{6,7},{7,6},{8,9},{9,8},{10,11... | collective-permute-start | bytes 294920 | tf_op jit(solution)/shard_map/ppermute | solution.py:496
  14.7 4.3 %collective-permute-start.5 = (f32[64,128]{1,0:T(8,128)S(1)}, f32[64,128]{1,0:T(8,128)S(1)}, u32[]{:S(2)}, u32[]{:S(2)}) collective-permute-start(f32[64,128]{1,0:T(8,128)S(1)} %get-tuple-element.114), channel_id=1, source_target_pairs={{0,7},{1,6},{2,5},{3,4},{4,3},{5,2},{6,1},{7,0},{8,15},{9,14},{10,... | collective-permute-start | bytes 98312 | tf_op jit(solution)/shard_map/ppermute | solution.py:496
  19.3 6.7 %collective-permute-start.7 = (f32[64,128]{1,0:T(8,128)S(1)}, f32[64,128]{1,0:T(8,128)S(1)}, u32[]{:S(2)}, u32[]{:S(2)}) collective-permute-start(f32[64,128]{1,0:T(8,128)S(1)} %get-tuple-element.116), channel_id=1, source_target_pairs={{0,16},{1,17},{2,18},{3,19},{4,20},{5,21},{6,22},{7,23},{8,24},{9,... | collective-permute-start | bytes 98312 | tf_op jit(solution)/shard_map/ppermute | solution.py:496
  21.9 5.6 %collective-permute-start.8 = (f32[64,128]{1,0:T(8,128)S(1)}, f32[64,128]{1,0:T(8,128)S(1)}, u32[]{:S(2)}, u32[]{:S(2)}) collective-permute-start(f32[64,128]{1,0:T(8,128)S(1)} %get-tuple-element.116), channel_id=1, source_target_pairs={{0,25},{1,24},{2,27},{3,26},{4,29},{5,28},{6,31},{7,30},{8,17},{9,... | collective-permute-start | bytes 98312 | tf_op jit(solution)/shard_map/ppermute | solution.py:496
  31.7 14.4 %collective-permute-start.10 = (f32[192,128]{1,0:T(8,128)S(1)}, f32[192,128]{1,0:T(8,128)S(1)}, u32[]{:S(2)}, u32[]{:S(2)}) collective-permute-start(f32[192,128]{1,0:T(8,128)S(1)} %get-tuple-element.120), channel_id=1, source_target_pairs={{0,1},{1,0},{2,3},{3,2},{4,5},{5,4},{6,7},{7,6},{8,9},{9,8},{10,11... | collective-permute-start | bytes 294920 | tf_op jit(solution)/shard_map/ppermute | solution.py:496
  33.6 4.2 %collective-permute-start.13 = (f32[64,128]{1,0:T(8,128)S(1)}, f32[64,128]{1,0:T(8,128)S(1)}, u32[]{:S(2)}, u32[]{:S(2)}) collective-permute-start(f32[64,128]{1,0:T(8,128)S(1)} %get-tuple-element.124), channel_id=1, source_target_pairs={{0,7},{1,6},{2,5},{3,4},{4,3},{5,2},{6,1},{7,0},{8,15},{9,14},{10,... | collective-permute-start | bytes 98312 | tf_op jit(solution)/shard_map/ppermute | solution.py:496
  38.4 4.8 %collective-permute-start.15 = (f32[64,128]{1,0:T(8,128)S(1)}, f32[64,128]{1,0:T(8,128)S(1)}, u32[]{:S(2)}, u32[]{:S(2)}) collective-permute-start(f32[64,128]{1,0:T(8,128)S(1)} %get-tuple-element.126), channel_id=1, source_target_pairs={{0,16},{1,17},{2,18},{3,19},{4,20},{5,21},{6,22},{7,23},{8,24},{9,... | collective-permute-start | bytes 98312 | tf_op jit(solution)/shard_map/ppermute | solution.py:496
  40.6 5.5 %collective-permute-start.16 = (f32[64,128]{1,0:T(8,128)S(1)}, f32[64,128]{1,0:T(8,128)S(1)}, u32[]{:S(2)}, u32[]{:S(2)}) collective-permute-start(f32[64,128]{1,0:T(8,128)S(1)} %get-tuple-element.126), channel_id=1, source_target_pairs={{0,25},{1,24},{2,27},{3,26},{4,29},{5,28},{6,31},{7,30},{8,17},{9,... | collective-permute-start | bytes 98312 | tf_op jit(solution)/shard_map/ppermute | solution.py:496
  50.1 14.5 %collective-permute-start.18 = (f32[192,128]{1,0:T(8,128)S(1)}, f32[192,128]{1,0:T(8,128)S(1)}, u32[]{:S(2)}, u32[]{:S(2)}) collective-permute-start(f32[192,128]{1,0:T(8,128)S(1)} %get-tuple-element.130), channel_id=1, source_target_pairs={{0,1},{1,0},{2,3},{3,2},{4,5},{5,4},{6,7},{7,6},{8,9},{9,8},{10,11... | collective-permute-start | bytes 294920 | tf_op jit(solution)/shard_map/ppermute | solution.py:496
  52.1 4.2 %collective-permute-start.21 = (f32[64,128]{1,0:T(8,128)S(1)}, f32[64,128]{1,0:T(8,128)S(1)}, u32[]{:S(2)}, u32[]{:S(2)}) collective-permute-start(f32[64,128]{1,0:T(8,128)S(1)} %get-tuple-element.133), channel_id=1, source_target_pairs={{0,7},{1,6},{2,5},{3,4},{4,3},{5,2},{6,1},{7,0},{8,15},{9,14},{10,... | collective-permute-start | bytes 98312 | tf_op jit(solution)/shard_map/ppermute | solution.py:496
  56.6 4.9 %collective-permute-start.23 = (f32[64,128]{1,0:T(8,128)S(1)}, f32[64,128]{1,0:T(8,128)S(1)}, u32[]{:S(2)}, u32[]{:S(2)}) collective-permute-start(f32[64,128]{1,0:T(8,128)S(1)} %get-tuple-element.135), channel_id=1, source_target_pairs={{0,16},{1,17},{2,18},{3,19},{4,20},{5,21},{6,22},{7,23},{8,24},{9,... | collective-permute-start | bytes 98312 | tf_op jit(solution)/shard_map/ppermute | solution.py:496
  59.1 5.5 %collective-permute-start.24 = (f32[64,128]{1,0:T(8,128)S(1)}, f32[64,128]{1,0:T(8,128)S(1)}, u32[]{:S(2)}, u32[]{:S(2)}) collective-permute-start(f32[64,128]{1,0:T(8,128)S(1)} %get-tuple-element.135), channel_id=1, source_target_pairs={{0,25},{1,24},{2,27},{3,26},{4,29},{5,28},{6,31},{7,30},{8,17},{9,... | collective-permute-start | bytes 98312 | tf_op jit(solution)/shard_map/ppermute | solution.py:496
  68.8 14.4 %collective-permute-start.26 = (f32[192,128]{1,0:T(8,128)S(1)}, f32[192,128]{1,0:T(8,128)S(1)}, u32[]{:S(2)}, u32[]{:S(2)}) collective-permute-start(f32[192,128]{1,0:T(8,128)S(1)} %get-tuple-element.139), channel_id=1, source_target_pairs={{0,1},{1,0},{2,3},{3,2},{4,5},{5,4},{6,7},{7,6},{8,9},{9,8},{10,11... | collective-permute-start | bytes 294920 | tf_op jit(solution)/shard_map/ppermute | solution.py:496
  75.3 4.9 %collective-permute-start.31 = (f32[64,128]{1,0:T(8,128)S(1)}, f32[64,128]{1,0:T(8,128)S(1)}, u32[]{:S(2)}, u32[]{:S(2)}) collective-permute-start(f32[64,128]{1,0:T(8,128)S(1)} %get-tuple-element.145), channel_id=1, source_target_pairs={{0,16},{1,17},{2,18},{3,19},{4,20},{5,21},{6,22},{7,23},{8,24},{9,... | collective-permute-start | bytes 98312 | tf_op jit(solution)/shard_map/ppermute | solution.py:496
  77.8 5.5 %collective-permute-start.32 = (f32[64,128]{1,0:T(8,128)S(1)}, f32[64,128]{1,0:T(8,128)S(1)}, u32[]{:S(2)}, u32[]{:S(2)}) collective-permute-start(f32[64,128]{1,0:T(8,128)S(1)} %get-tuple-element.145), channel_id=1, source_target_pairs={{0,25},{1,24},{2,27},{3,26},{4,29},{5,28},{6,31},{7,30},{8,17},{9,... | collective-permute-start | bytes 98312 | tf_op jit(solution)/shard_map/ppermute | solution.py:496
  87.2 14.5 %collective-permute-start.34 = (f32[192,128]{1,0:T(8,128)S(1)}, f32[192,128]{1,0:T(8,128)S(1)}, u32[]{:S(2)}, u32[]{:S(2)}) collective-permute-start(f32[192,128]{1,0:T(8,128)S(1)} %get-tuple-element.149), channel_id=1, source_target_pairs={{0,1},{1,0},{2,3},{3,2},{4,5},{5,4},{6,7},{7,6},{8,9},{9,8},{10,11... | collective-permute-start | bytes 294920 | tf_op jit(solution)/shard_map/ppermute | solution.py:496
  89.3 4.2 %collective-permute-start.37 = (f32[64,128]{1,0:T(8,128)S(1)}, f32[64,128]{1,0:T(8,128)S(1)}, u32[]{:S(2)}, u32[]{:S(2)}) collective-permute-start(f32[64,128]{1,0:T(8,128)S(1)} %get-tuple-element.152), channel_id=1, source_target_pairs={{0,7},{1,6},{2,5},{3,4},{4,3},{5,2},{6,1},{7,0},{8,15},{9,14},{10,... | collective-permute-start | bytes 98312 | tf_op jit(solution)/shard_map/ppermute | solution.py:496
  93.8 4.9 %collective-permute-start.39 = (f32[64,128]{1,0:T(8,128)S(1)}, f32[64,128]{1,0:T(8,128)S(1)}, u32[]{:S(2)}, u32[]{:S(2)}) collective-permute-start(f32[64,128]{1,0:T(8,128)S(1)} %get-tuple-element.154), channel_id=1, source_target_pairs={{0,16},{1,17},{2,18},{3,19},{4,20},{5,21},{6,22},{7,23},{8,24},{9,... | collective-permute-start | bytes 98312 | tf_op jit(solution)/shard_map/ppermute | solution.py:496
  96.3 5.5 %collective-permute-start.40 = (f32[64,128]{1,0:T(8,128)S(1)}, f32[64,128]{1,0:T(8,128)S(1)}, u32[]{:S(2)}, u32[]{:S(2)}) collective-permute-start(f32[64,128]{1,0:T(8,128)S(1)} %get-tuple-element.154), channel_id=1, source_target_pairs={{0,25},{1,24},{2,27},{3,26},{4,29},{5,28},{6,31},{7,30},{8,17},{9,... | collective-permute-start | bytes 98312 | tf_op jit(solution)/shard_map/ppermute | solution.py:496
  106.0 14.4 %collective-permute-start.42 = (f32[192,128]{1,0:T(8,128)S(1)}, f32[192,128]{1,0:T(8,128)S(1)}, u32[]{:S(2)}, u32[]{:S(2)}) collective-permute-start(f32[192,128]{1,0:T(8,128)S(1)} %get-tuple-element.158), channel_id=1, source_target_pairs={{0,1},{1,0},{2,3},{3,2},{4,5},{5,4},{6,7},{7,6},{8,9},{9,8},{10,11... | collective-permute-start | bytes 294920 | tf_op jit(solution)/shard_map/ppermute | solution.py:496
  107.9 4.2 %collective-permute-start.45 = (f32[64,128]{1,0:T(8,128)S(1)}, f32[64,128]{1,0:T(8,128)S(1)}, u32[]{:S(2)}, u32[]{:S(2)}) collective-permute-start(f32[64,128]{1,0:T(8,128)S(1)} %get-tuple-element.161), channel_id=1, source_target_pairs={{0,7},{1,6},{2,5},{3,4},{4,3},{5,2},{6,1},{7,0},{8,15},{9,14},{10,... | collective-permute-start | bytes 98312 | tf_op jit(solution)/shard_map/ppermute | solution.py:496
  112.4 4.9 %collective-permute-start.47 = (f32[64,128]{1,0:T(8,128)S(1)}, f32[64,128]{1,0:T(8,128)S(1)}, u32[]{:S(2)}, u32[]{:S(2)}) collective-permute-start(f32[64,128]{1,0:T(8,128)S(1)} %get-tuple-element.163), channel_id=1, source_target_pairs={{0,16},{1,17},{2,18},{3,19},{4,20},{5,21},{6,22},{7,23},{8,24},{9,... | collective-permute-start | bytes 98312 | tf_op jit(solution)/shard_map/ppermute | solution.py:496
  114.9 5.5 %collective-permute-start.48 = (f32[64,128]{1,0:T(8,128)S(1)}, f32[64,128]{1,0:T(8,128)S(1)}, u32[]{:S(2)}, u32[]{:S(2)}) collective-permute-start(f32[64,128]{1,0:T(8,128)S(1)} %get-tuple-element.163), channel_id=1, source_target_pairs={{0,25},{1,24},{2,27},{3,26},{4,29},{5,28},{6,31},{7,30},{8,17},{9,... | collective-permute-start | bytes 98312 | tf_op jit(solution)/shard_map/ppermute | solution.py:496
  120.8 5.9 %collective-permute-start.51 = (f32[64,128]{1,0:T(8,128)S(1)}, f32[64,128]{1,0:T(8,128)S(1)}, u32[]{:S(2)}, u32[]{:S(2)}) collective-permute-start(f32[64,128]{1,0:T(8,128)S(1)} %get-tuple-element.170), channel_id=1, source_target_pairs={{0,5},{1,4},{2,7},{3,6},{4,1},{5,0},{6,3},{7,2},{8,13},{9,12},{10,... | collective-permute-start | bytes 98312 | tf_op jit(solution)/shard_map/ppermute | solution.py:496
  121.4 5.3 %collective-permute-start.52 = (f32[64,128]{1,0:T(8,128)S(1)}, f32[64,128]{1,0:T(8,128)S(1)}, u32[]{:S(2)}, u32[]{:S(2)}) collective-permute-start(f32[64,128]{1,0:T(8,128)S(1)} %get-tuple-element.170), channel_id=1, source_target_pairs={{0,7},{1,6},{2,5},{3,4},{4,3},{5,2},{6,1},{7,0},{8,15},{9,14},{10,... | collective-permute-start | bytes 98312 | tf_op jit(solution)/shard_map/ppermute | solution.py:496
  127.0 4.9 %collective-permute-start.55 = (f32[72,128]{1,0:T(8,128)S(1)}, f32[72,128]{1,0:T(8,128)S(1)}, u32[]{:S(2)}, u32[]{:S(2)}) collective-permute-start(f32[72,128]{1,0:T(8,128)S(1)} %get-tuple-element.173), channel_id=1, source_target_pairs={{0,16},{1,17},{2,18},{3,19},{4,20},{5,21},{6,22},{7,23},{8,24},{9,... | collective-permute-start | bytes 110600 | tf_op jit(solution)/shard_map/ppermute | solution.py:496
  129.0 5.2 %collective-permute-start.56 = (f32[72,128]{1,0:T(8,128)S(1)}, f32[72,128]{1,0:T(8,128)S(1)}, u32[]{:S(2)}, u32[]{:S(2)}) collective-permute-start(f32[72,128]{1,0:T(8,128)S(1)} %get-tuple-element.173), channel_id=1, source_target_pairs={{0,25},{1,24},{2,27},{3,26},{4,29},{5,28},{6,31},{7,30},{8,17},{9,... | collective-permute-start | bytes 110600 | tf_op jit(solution)/shard_map/ppermute | solution.py:496
  134.3 4.8 %collective-permute-start.60 = (f32[8,128]{1,0:T(8,128)S(1)}, f32[8,128]{1,0:T(8,128)S(1)}, u32[]{:S(2)}, u32[]{:S(2)}) collective-permute-start(f32[8,128]{1,0:T(8,128)S(1)} %slice_add_fusion), channel_id=1, source_target_pairs={{0,7},{1,6},{2,5},{3,4},{4,3},{5,2},{6,1},{7,0},{8,15},{9,14},{10,... | collective-permute-start | bytes 12296 | tf_op jit(solution)/shard_map/ppermute | solution.py:496
  (32 other events, 115.4 us)
where the time goes:
time: 143 us
  starting transfers between devices  56.5 us (40%)
  waiting for transfers between devices  54.3 us (38%)
  Pallas kernels  30.5 us (21%)
    ppermute x61, starting transfers between devices, swap(): return lax.ppermute(value, ('rows', 'leaf'), pairs)  56.5 us
    ppermute x61, waiting for transfers between devices, swap(): return lax.ppermute(value, ('rows', 'leaf'), pairs)  54.3 us
    pallas_call x34, Pallas kernels, call(): pl.pallas_call(kernel, out_shape=[jax.ShapeDtypeStruct(shape, dtype) for...  30.5 us
  transfers between devices with their start and end apart: 61, of which 37 were waited for; matrix products, arithmetic and copies ran while one was open for 0% of the time, Pallas kernels for 8%

commit v1 on v0

--- a/solution.py
+++ b/solution.py
@@ -341,8 +341,9 @@
             parts.append(refs[place + 1][:half] + refs[place + 2][:half])
         place += size
     value = jnp.concatenate(parts, axis=1)
-    total = table_right(member, value, (table_ref[0, member], table_ref[1, member]))
-    refs[-1][...] = total[:, rank:]
+    table = (table_ref[0, member, :, rank:], table_ref[1, member, :, rank:])
+    feed = mm(value.astype(BF16), table_ref[0, member, :, :rank])
+    refs[-1][...] = table_right(member, value, table)
     if last:
         sums = None
         for ref in refs[:count]:
@@ -350,7 +351,7 @@
                 sums = ref[half:] if sums is None else sums + ref[half:]
         refs[count][...] = sums
     else:
-        value = keep_ref[...] + got_ref[rank:] + total[:, :rank]
+        value = keep_ref[...] + got_ref[rank:] + feed
         refs[count][...] = value
         if len(refs) == count + 3:
             refs[count + 1][...] = chain_right(1 - member, value, upper_ref[1 - member, 0, 0])

time: 143 us -> 143 us (level)
  no operation moved by 1% of the time
where the time goes in v1:
time: 143 us
  starting transfers between devices  56.8 us (40%)
  waiting for transfers between devices  54.3 us (38%)
  Pallas kernels  30.3 us (21%)
    ppermute x61, starting transfers between devices, swap(): return lax.ppermute(value, ('rows', 'leaf'), pairs)  56.8 us
    ppermute x61, waiting for transfers between devices, swap(): return lax.ppermute(value, ('rows', 'leaf'), pairs)  54.3 us
    pallas_call x34, Pallas kernels, call(): pl.pallas_call(kernel, out_shape=[jax.ShapeDtypeStruct(shape, dtype) for...  30.3 us
  transfers between devices with their start and end apart: 61, of which 37 were waited for; matrix products, arithmetic and copies ran while one was open for 0% of the time, Pallas kernels for 8%

profile of v1, /device:TPU:0, one launch (start us, length us, event | category | flops | bytes accessed | tf_op | source)
XLA Modules:
  0.0 142.8 jit_solution(7551774714816043824)
XLA Ops:
  0.6 2.3 %shard_map.77 = (f32[1024,128]{1,0:T(8,128)S(1)}, f32[1024,128]{1,0:T(8,128)S(1)}, bf16[4,512,128]{2,1,0:T(8,128)(2,1)S(1)}, bf16[4,512,128]{2,1,0:T(8,128)(2,1)...) custom-call(f32[2048,128]{1,0:T(8,128)} %refs_0_.7, ...), custom_call_target="tpu_custom_call" | custom-call | flops 629145600 | tf_op jit(solution)/shard_map/pallas_call | solution.py:81
  3.5 4.2 %shard_map.78 = (bf16[4,128,512]{2,1,0:T(8,128)(2,1)S(1)}, bf16[2,256,512]{2,1,0:T(8,128)(2,1)S(1)}, bf16[2,2,512,640]{3,2,1,0:T(8,128)(2,1)S(1)}, bf16[2,2,512,...) custom-call(bf16[7,3,128,128]{3,2,1,0:T(8,128)(2,1)S(1)} %get-tuple-element.90.refs_0_, ...), custom_call_target="tpu_custom_call" | custom-call | flops 1258291200 | tf_op jit(solution)/shard_map/pallas_call | solution.py:81
  8.0 3.0 %collective-permute-start.3 = (f32[320,128]{1,0:T(8,128)S(1)}, f32[320,128]{1,0:T(8,128)S(1)}, u32[]{:S(2)}, u32[]{:S(2)}) collective-permute-start(f32[320,128]{1,0:T(8,128)S(1)} %get-tuple-element.112.own_ref), channel_id=1, source_target_pairs={{0,2},{1,3},{2,0},{3,1},{4,6},{5,7},{6,4},{7,5},{8,10},{9,11},{10,... | collective-permute-start | bytes 491528 | tf_op jit(solution)/shard_map/ppermute | solution.py:497
  15.4 2.1 %collective-permute-done.4.far_ref.refs_1_ = f32[320,128]{1,0:T(8,128)S(1)} collective-permute-done((f32[320,128]{1,0:T(8,128)S(1)}, f32[320,128]{1,0:T(8,128)S(1)}, u32[]{:S(2)}, u32[]{:S(2)}) %collective-permute-start.4) | collective-permute-done | bytes 163872 | tf_op jit(solution)/shard_map/ppermute | solution.py:497
  19.3 2.6 %collective-permute-start.7 = (f32[64,128]{1,0:T(8,128)S(1)}, f32[64,128]{1,0:T(8,128)S(1)}, u32[]{:S(2)}, u32[]{:S(2)}) collective-permute-start(f32[64,128]{1,0:T(8,128)S(1)} %get-tuple-element.116), channel_id=1, source_target_pairs={{0,16},{1,17},{2,18},{3,19},{4,20},{5,21},{6,22},{7,23},{8,24},{9,... | collective-permute-start | bytes 98312 | tf_op jit(solution)/shard_map/ppermute | solution.py:497
  24.0 2.0 %collective-permute-done.6.refs_3_ = f32[64,128]{1,0:T(8,128)S(1)} collective-permute-done((f32[64,128]{1,0:T(8,128)S(1)}, f32[64,128]{1,0:T(8,128)S(1)}, u32[]{:S(2)}, u32[]{:S(2)}) %collective-permute-start.6) | collective-permute-done | bytes 32800 | tf_op jit(solution)/shard_map/ppermute | solution.py:497
  29.0 2.1 %shard_map.86 = (f32[2048,128]{1,0:T(8,128)S(1)}, f32[2048,128]{1,0:T(8,128)S(1)}) custom-call(bf16[2,4,512,512]{3,2,1,0:T(8,128)(2,1)S(1)} %copy-done, bf16[4,512,128]{2,1,0:T(8,128)(2,1)S(1)} %get-tuple-element.92.refs_2_.refs_1_.refs_7_.u_ref, bf16[2,2,512,640]{3,2,1,0:T(8,128)(2,1)S(1)} %get-tuple-element.97.refs_2_.wide_ref, ...), custom_call_target="tpu_custom_call" | custom-call | flops 838860800 | tf_op jit(solution)/shard_map/pallas_call | solution.py:81
  33.6 1.5 %collective-permute-start.13 = (f32[64,128]{1,0:T(8,128)S(1)}, f32[64,128]{1,0:T(8,128)S(1)}, u32[]{:S(2)}, u32[]{:S(2)}) collective-permute-start(f32[64,128]{1,0:T(8,128)S(1)} %get-tuple-element.124), channel_id=1, source_target_pairs={{0,7},{1,6},{2,5},{3,4},{4,3},{5,2},{6,1},{7,0},{8,15},{9,14},{10,... | collective-permute-start | bytes 98312 | tf_op jit(solution)/shard_map/ppermute | solution.py:497
  35.8 2.0 %collective-permute-done.13.refs_2_ = f32[64,128]{1,0:T(8,128)S(1)} collective-permute-done((f32[64,128]{1,0:T(8,128)S(1)}, f32[64,128]{1,0:T(8,128)S(1)}, u32[]{:S(2)}, u32[]{:S(2)}) %collective-permute-start.13) | collective-permute-done | bytes 32800 | tf_op jit(solution)/shard_map/ppermute | solution.py:497
  38.4 2.3 %collective-permute-start.15 = (f32[64,128]{1,0:T(8,128)S(1)}, f32[64,128]{1,0:T(8,128)S(1)}, u32[]{:S(2)}, u32[]{:S(2)}) collective-permute-start(f32[64,128]{1,0:T(8,128)S(1)} %get-tuple-element.126), channel_id=1, source_target_pairs={{0,16},{1,17},{2,18},{3,19},{4,20},{5,21},{6,22},{7,23},{8,24},{9,... | collective-permute-start | bytes 98312 | tf_op jit(solution)/shard_map/ppermute | solution.py:497
  43.2 2.9 %collective-permute-done.16.refs_5_ = f32[64,128]{1,0:T(8,128)S(1)} collective-permute-done((f32[64,128]{1,0:T(8,128)S(1)}, f32[64,128]{1,0:T(8,128)S(1)}, u32[]{:S(2)}, u32[]{:S(2)}) %collective-permute-start.16) | collective-permute-done | bytes 32800 | tf_op jit(solution)/shard_map/ppermute | solution.py:497
  47.6 1.9 %shard_map.90 = (f32[2048,128]{1,0:T(8,128)S(1)}, f32[1,128]{1,0:T(1,128)S(1)}) custom-call(bf16[2,4,512,512]{3,2,1,0:T(8,128)(2,1)S(1)} %copy-done, bf16[4,512,128]{2,1,0:T(8,128)(2,1)S(1)} %get-tuple-element.89.refs_3_.refs_1_.refs_8_.u_ref, bf16[2,2,512,640]{3,2,1,0:T(8,128)(2,1)S(1)} %get-tuple-element.97.refs_2_.wide_ref, ...), custom_call_target="tpu_custom_call" | custom-call | flops 838860800 | tf_op jit(solution)/shard_map/pallas_call | solution.py:81
  54.3 2.0 %collective-permute-done.21.refs_2_ = f32[64,128]{1,0:T(8,128)S(1)} collective-permute-done((f32[64,128]{1,0:T(8,128)S(1)}, f32[64,128]{1,0:T(8,128)S(1)}, u32[]{:S(2)}, u32[]{:S(2)}) %collective-permute-start.21) | collective-permute-done | bytes 32800 | tf_op jit(solution)/shard_map/ppermute | solution.py:497
  56.6 2.5 %collective-permute-start.23 = (f32[64,128]{1,0:T(8,128)S(1)}, f32[64,128]{1,0:T(8,128)S(1)}, u32[]{:S(2)}, u32[]{:S(2)}) collective-permute-start(f32[64,128]{1,0:T(8,128)S(1)} %get-tuple-element.135), channel_id=1, source_target_pairs={{0,16},{1,17},{2,18},{3,19},{4,20},{5,21},{6,22},{7,23},{8,24},{9,... | collective-permute-start | bytes 98312 | tf_op jit(solution)/shard_map/ppermute | solution.py:497
  61.5 3.1 %collective-permute-done.24.refs_5_ = f32[64,128]{1,0:T(8,128)S(1)} collective-permute-done((f32[64,128]{1,0:T(8,128)S(1)}, f32[64,128]{1,0:T(8,128)S(1)}, u32[]{:S(2)}, u32[]{:S(2)}) %collective-permute-start.24) | collective-permute-done | bytes 32800 | tf_op jit(solution)/shard_map/ppermute | solution.py:497
  66.3 2.1 %shard_map.94 = (f32[2048,128]{1,0:T(8,128)S(1)}, f32[2048,128]{1,0:T(8,128)S(1)}) custom-call(bf16[2,4,512,512]{3,2,1,0:T(8,128)(2,1)S(1)} %copy-done, bf16[4,512,128]{2,1,0:T(8,128)(2,1)S(1)} %get-tuple-element.92.refs_2_.refs_1_.refs_7_.u_ref, bf16[2,2,512,640]{3,2,1,0:T(8,128)(2,1)S(1)} %get-tuple-element.97.refs_2_.wide_ref, ...), custom_call_target="tpu_custom_call" | custom-call | flops 838860800 | tf_op jit(solution)/shard_map/pallas_call | solution.py:81
  73.1 2.0 %collective-permute-done.29.refs_2_ = f32[64,128]{1,0:T(8,128)S(1)} collective-permute-done((f32[64,128]{1,0:T(8,128)S(1)}, f32[64,128]{1,0:T(8,128)S(1)}, u32[]{:S(2)}, u32[]{:S(2)}) %collective-permute-start.29) | collective-permute-done | bytes 32800 | tf_op jit(solution)/shard_map/ppermute | solution.py:497
  75.4 2.5 %collective-permute-start.31 = (f32[64,128]{1,0:T(8,128)S(1)}, f32[64,128]{1,0:T(8,128)S(1)}, u32[]{:S(2)}, u32[]{:S(2)}) collective-permute-start(f32[64,128]{1,0:T(8,128)S(1)} %get-tuple-element.145), channel_id=1, source_target_pairs={{0,16},{1,17},{2,18},{3,19},{4,20},{5,21},{6,22},{7,23},{8,24},{9,... | collective-permute-start | bytes 98312 | tf_op jit(solution)/shard_map/ppermute | solution.py:497
  80.3 3.0 %collective-permute-done.32.refs_5_ = f32[64,128]{1,0:T(8,128)S(1)} collective-permute-done((f32[64,128]{1,0:T(8,128)S(1)}, f32[64,128]{1,0:T(8,128)S(1)}, u32[]{:S(2)}, u32[]{:S(2)}) %collective-permute-start.32) | collective-permute-done | bytes 32800 | tf_op jit(solution)/shard_map/ppermute | solution.py:497
  84.8 1.9 %shard_map.98 = (f32[2048,128]{1,0:T(8,128)S(1)}, f32[1,128]{1,0:T(1,128)S(1)}) custom-call(bf16[2,4,512,512]{3,2,1,0:T(8,128)(2,1)S(1)} %copy-done, bf16[4,512,128]{2,1,0:T(8,128)(2,1)S(1)} %get-tuple-element.89.refs_3_.refs_1_.refs_8_.u_ref, bf16[2,2,512,640]{3,2,1,0:T(8,128)(2,1)S(1)} %get-tuple-element.97.refs_2_.wide_ref, ...), custom_call_target="tpu_custom_call" | custom-call | flops 838860800 | tf_op jit(solution)/shard_map/pallas_call | solution.py:81
  91.6 2.0 %collective-permute-done.37.refs_2_ = f32[64,128]{1,0:T(8,128)S(1)} collective-permute-done((f32[64,128]{1,0:T(8,128)S(1)}, f32[64,128]{1,0:T(8,128)S(1)}, u32[]{:S(2)}, u32[]{:S(2)}) %collective-permute-start.37) | collective-permute-done | bytes 32800 | tf_op jit(solution)/shard_map/ppermute | solution.py:497
  93.9 2.5 %collective-permute-start.39 = (f32[64,128]{1,0:T(8,128)S(1)}, f32[64,128]{1,0:T(8,128)S(1)}, u32[]{:S(2)}, u32[]{:S(2)}) collective-permute-start(f32[64,128]{1,0:T(8,128)S(1)} %get-tuple-element.154), channel_id=1, source_target_pairs={{0,16},{1,17},{2,18},{3,19},{4,20},{5,21},{6,22},{7,23},{8,24},{9,... | collective-permute-start | bytes 98312 | tf_op jit(solution)/shard_map/ppermute | solution.py:497
  98.7 3.1 %collective-permute-done.40.refs_5_ = f32[64,128]{1,0:T(8,128)S(1)} collective-permute-done((f32[64,128]{1,0:T(8,128)S(1)}, f32[64,128]{1,0:T(8,128)S(1)}, u32[]{:S(2)}, u32[]{:S(2)}) %collective-permute-start.40) | collective-permute-done | bytes 32800 | tf_op jit(solution)/shard_map/ppermute | solution.py:497
  103.4 2.1 %shard_map.102 = (f32[2048,128]{1,0:T(8,128)S(1)}, f32[2048,128]{1,0:T(8,128)S(1)}) custom-call(bf16[2,4,512,512]{3,2,1,0:T(8,128)(2,1)S(1)} %copy-done, bf16[4,512,128]{2,1,0:T(8,128)(2,1)S(1)} %get-tuple-element.92.refs_2_.refs_1_.refs_7_.u_ref, bf16[2,2,512,640]{3,2,1,0:T(8,128)(2,1)S(1)} %get-tuple-element.97.refs_2_.wide_ref, ...), custom_call_target="tpu_custom_call" | custom-call | flops 838860800 | tf_op jit(solution)/shard_map/pallas_call | solution.py:81
  110.2 2.0 %collective-permute-done.45.refs_2_ = f32[64,128]{1,0:T(8,128)S(1)} collective-permute-done((f32[64,128]{1,0:T(8,128)S(1)}, f32[64,128]{1,0:T(8,128)S(1)}, u32[]{:S(2)}, u32[]{:S(2)}) %collective-permute-start.45) | collective-permute-done | bytes 32800 | tf_op jit(solution)/shard_map/ppermute | solution.py:497
  112.5 2.5 %collective-permute-start.47 = (f32[64,128]{1,0:T(8,128)S(1)}, f32[64,128]{1,0:T(8,128)S(1)}, u32[]{:S(2)}, u32[]{:S(2)}) collective-permute-start(f32[64,128]{1,0:T(8,128)S(1)} %get-tuple-element.163), channel_id=1, source_target_pairs={{0,16},{1,17},{2,18},{3,19},{4,20},{5,21},{6,22},{7,23},{8,24},{9,... | collective-permute-start | bytes 98312 | tf_op jit(solution)/shard_map/ppermute | solution.py:497
  117.4 3.0 %collective-permute-done.48.refs_5_ = f32[64,128]{1,0:T(8,128)S(1)} collective-permute-done((f32[64,128]{1,0:T(8,128)S(1)}, f32[64,128]{1,0:T(8,128)S(1)}, u32[]{:S(2)}, u32[]{:S(2)}) %collective-permute-start.48) | collective-permute-done | bytes 32800 | tf_op jit(solution)/shard_map/ppermute | solution.py:497
  125.0 1.8 %collective-permute-done.50.refs_0_ = f32[64,128]{1,0:T(8,128)S(1)} collective-permute-done((f32[64,128]{1,0:T(8,128)S(1)}, f32[64,128]{1,0:T(8,128)S(1)}, u32[]{:S(2)}, u32[]{:S(2)}) %collective-permute-start.50) | collective-permute-done | bytes 32800 | tf_op jit(solution)/shard_map/ppermute | solution.py:497
  127.0 2.0 %collective-permute-start.55 = (f32[72,128]{1,0:T(8,128)S(1)}, f32[72,128]{1,0:T(8,128)S(1)}, u32[]{:S(2)}, u32[]{:S(2)}) collective-permute-start(f32[72,128]{1,0:T(8,128)S(1)} %get-tuple-element.173), channel_id=1, source_target_pairs={{0,16},{1,17},{2,18},{3,19},{4,20},{5,21},{6,22},{7,23},{8,24},{9,... | collective-permute-start | bytes 110600 | tf_op jit(solution)/shard_map/ppermute | solution.py:497
  129.0 1.8 %collective-permute-start.56 = (f32[72,128]{1,0:T(8,128)S(1)}, f32[72,128]{1,0:T(8,128)S(1)}, u32[]{:S(2)}, u32[]{:S(2)}) collective-permute-start(f32[72,128]{1,0:T(8,128)S(1)} %get-tuple-element.173), channel_id=1, source_target_pairs={{0,25},{1,24},{2,27},{3,26},{4,29},{5,28},{6,31},{7,30},{8,17},{9,... | collective-permute-start | bytes 110600 | tf_op jit(solution)/shard_map/ppermute | solution.py:497
  131.9 2.3 %collective-permute-done.56.refs_5_ = f32[72,128]{1,0:T(8,128)S(1)} collective-permute-done((f32[72,128]{1,0:T(8,128)S(1)}, f32[72,128]{1,0:T(8,128)S(1)}, u32[]{:S(2)}, u32[]{:S(2)}) %collective-permute-start.56) | collective-permute-done | bytes 36896 | tf_op jit(solution)/shard_map/ppermute | solution.py:497
  139.2 1.5 %collective-permute-done.58 = f32[8,128]{1,0:T(8,128)S(1)} collective-permute-done((f32[8,128]{1,0:T(8,128)S(1)}, f32[8,128]{1,0:T(8,128)S(1)}, u32[]{:S(2)}, u32[]{:S(2)}) %collective-permute-start.58) | collective-permute-done | bytes 4128 | tf_op jit(solution)/shard_map/ppermute | solution.py:497
  (133 shorter events, 67.5 us)
Async XLA Ops:
  3.0 4.9 %collective-permute-start = (f32[192,128]{1,0:T(8,128)S(1)}, f32[192,128]{1,0:T(8,128)S(1)}, u32[]{:S(2)}, u32[]{:S(2)}) collective-permute-start(f32[192,128]{1,0:T(8,128)S(1)} %get-tuple-element.99), channel_id=1, source_target_pairs={{0,1},{1,0},{2,3},{3,2},{4,5},{5,4},{6,7},{7,6},{8,9},{9,8},{10,11... | collective-permute-start | bytes 294920 | tf_op jit(solution)/shard_map/ppermute | solution.py:497
  7.8 15.1 %collective-permute-start.2 = (f32[4,128,128]{2,1,0:T(8,128)S(1)}, f32[4,128,128]{2,1,0:T(8,128)S(1)}, u32[]{:S(2)}, u32[]{:S(2)}) collective-permute-start(f32[4,128,128]{2,1,0:T(8,128)S(1)} %get-tuple-element.107.chip_ref), channel_id=1, source_target_pairs={{0,1},{1,0},{2,3},{3,2},{4,5},{5,4},{6,7},{7,6},{8,9},{9,8},{10,11... | collective-permute-start | bytes 786440 | tf_op jit(solution)/shard_map/ppermute | solution.py:497
  8.0 7.4 %collective-permute-start.3 = (f32[320,128]{1,0:T(8,128)S(1)}, f32[320,128]{1,0:T(8,128)S(1)}, u32[]{:S(2)}, u32[]{:S(2)}) collective-permute-start(f32[320,128]{1,0:T(8,128)S(1)} %get-tuple-element.112.own_ref), channel_id=1, source_target_pairs={{0,2},{1,3},{2,0},{3,1},{4,6},{5,7},{6,4},{7,5},{8,10},{9,11},{10,... | collective-permute-start | bytes 491528 | tf_op jit(solution)/shard_map/ppermute | solution.py:497
  11.0 6.5 %collective-permute-start.4 = (f32[320,128]{1,0:T(8,128)S(1)}, f32[320,128]{1,0:T(8,128)S(1)}, u32[]{:S(2)}, u32[]{:S(2)}) collective-permute-start(f32[320,128]{1,0:T(8,128)S(1)} %get-tuple-element.113), channel_id=1, source_target_pairs={{0,5},{1,4},{2,7},{3,6},{4,1},{5,0},{6,3},{7,2},{8,13},{9,12},{10,... | collective-permute-start | bytes 491528 | tf_op jit(solution)/shard_map/ppermute | solution.py:497
  13.9 10.1 %collective-permute-start.1 = (f32[192,128]{1,0:T(8,128)S(1)}, f32[192,128]{1,0:T(8,128)S(1)}, u32[]{:S(2)}, u32[]{:S(2)}) collective-permute-start(f32[192,128]{1,0:T(8,128)S(1)} %get-tuple-element.105), channel_id=1, source_target_pairs={{0,1},{1,0},{2,3},{3,2},{4,5},{5,4},{6,7},{7,6},{8,9},{9,8},{10,11... | collective-permute-start | bytes 294920 | tf_op jit(solution)/shard_map/ppermute | solution.py:497
  14.7 4.3 %collective-permute-start.5 = (f32[64,128]{1,0:T(8,128)S(1)}, f32[64,128]{1,0:T(8,128)S(1)}, u32[]{:S(2)}, u32[]{:S(2)}) collective-permute-start(f32[64,128]{1,0:T(8,128)S(1)} %get-tuple-element.114), channel_id=1, source_target_pairs={{0,7},{1,6},{2,5},{3,4},{4,3},{5,2},{6,1},{7,0},{8,15},{9,14},{10,... | collective-permute-start | bytes 98312 | tf_op jit(solution)/shard_map/ppermute | solution.py:497
  19.3 6.7 %collective-permute-start.7 = (f32[64,128]{1,0:T(8,128)S(1)}, f32[64,128]{1,0:T(8,128)S(1)}, u32[]{:S(2)}, u32[]{:S(2)}) collective-permute-start(f32[64,128]{1,0:T(8,128)S(1)} %get-tuple-element.116), channel_id=1, source_target_pairs={{0,16},{1,17},{2,18},{3,19},{4,20},{5,21},{6,22},{7,23},{8,24},{9,... | collective-permute-start | bytes 98312 | tf_op jit(solution)/shard_map/ppermute | solution.py:497
  21.9 5.6 %collective-permute-start.8 = (f32[64,128]{1,0:T(8,128)S(1)}, f32[64,128]{1,0:T(8,128)S(1)}, u32[]{:S(2)}, u32[]{:S(2)}) collective-permute-start(f32[64,128]{1,0:T(8,128)S(1)} %get-tuple-element.116), channel_id=1, source_target_pairs={{0,25},{1,24},{2,27},{3,26},{4,29},{5,28},{6,31},{7,30},{8,17},{9,... | collective-permute-start | bytes 98312 | tf_op jit(solution)/shard_map/ppermute | solution.py:497
  31.6 14.4 %collective-permute-start.10 = (f32[192,128]{1,0:T(8,128)S(1)}, f32[192,128]{1,0:T(8,128)S(1)}, u32[]{:S(2)}, u32[]{:S(2)}) collective-permute-start(f32[192,128]{1,0:T(8,128)S(1)} %get-tuple-element.120), channel_id=1, source_target_pairs={{0,1},{1,0},{2,3},{3,2},{4,5},{5,4},{6,7},{7,6},{8,9},{9,8},{10,11... | collective-permute-start | bytes 294920 | tf_op jit(solution)/shard_map/ppermute | solution.py:497
  33.6 4.2 %collective-permute-start.13 = (f32[64,128]{1,0:T(8,128)S(1)}, f32[64,128]{1,0:T(8,128)S(1)}, u32[]{:S(2)}, u32[]{:S(2)}) collective-permute-start(f32[64,128]{1,0:T(8,128)S(1)} %get-tuple-element.124), channel_id=1, source_target_pairs={{0,7},{1,6},{2,5},{3,4},{4,3},{5,2},{6,1},{7,0},{8,15},{9,14},{10,... | collective-permute-start | bytes 98312 | tf_op jit(solution)/shard_map/ppermute | solution.py:497
  38.4 4.8 %collective-permute-start.15 = (f32[64,128]{1,0:T(8,128)S(1)}, f32[64,128]{1,0:T(8,128)S(1)}, u32[]{:S(2)}, u32[]{:S(2)}) collective-permute-start(f32[64,128]{1,0:T(8,128)S(1)} %get-tuple-element.126), channel_id=1, source_target_pairs={{0,16},{1,17},{2,18},{3,19},{4,20},{5,21},{6,22},{7,23},{8,24},{9,... | collective-permute-start | bytes 98312 | tf_op jit(solution)/shard_map/ppermute | solution.py:497
  40.6 5.5 %collective-permute-start.16 = (f32[64,128]{1,0:T(8,128)S(1)}, f32[64,128]{1,0:T(8,128)S(1)}, u32[]{:S(2)}, u32[]{:S(2)}) collective-permute-start(f32[64,128]{1,0:T(8,128)S(1)} %get-tuple-element.126), channel_id=1, source_target_pairs={{0,25},{1,24},{2,27},{3,26},{4,29},{5,28},{6,31},{7,30},{8,17},{9,... | collective-permute-start | bytes 98312 | tf_op jit(solution)/shard_map/ppermute | solution.py:497
  50.1 14.5 %collective-permute-start.18 = (f32[192,128]{1,0:T(8,128)S(1)}, f32[192,128]{1,0:T(8,128)S(1)}, u32[]{:S(2)}, u32[]{:S(2)}) collective-permute-start(f32[192,128]{1,0:T(8,128)S(1)} %get-tuple-element.130), channel_id=1, source_target_pairs={{0,1},{1,0},{2,3},{3,2},{4,5},{5,4},{6,7},{7,6},{8,9},{9,8},{10,11... | collective-permute-start | bytes 294920 | tf_op jit(solution)/shard_map/ppermute | solution.py:497
  52.1 4.2 %collective-permute-start.21 = (f32[64,128]{1,0:T(8,128)S(1)}, f32[64,128]{1,0:T(8,128)S(1)}, u32[]{:S(2)}, u32[]{:S(2)}) collective-permute-start(f32[64,128]{1,0:T(8,128)S(1)} %get-tuple-element.133), channel_id=1, source_target_pairs={{0,7},{1,6},{2,5},{3,4},{4,3},{5,2},{6,1},{7,0},{8,15},{9,14},{10,... | collective-permute-start | bytes 98312 | tf_op jit(solution)/shard_map/ppermute | solution.py:497
  56.6 4.9 %collective-permute-start.23 = (f32[64,128]{1,0:T(8,128)S(1)}, f32[64,128]{1,0:T(8,128)S(1)}, u32[]{:S(2)}, u32[]{:S(2)}) collective-permute-start(f32[64,128]{1,0:T(8,128)S(1)} %get-tuple-element.135), channel_id=1, source_target_pairs={{0,16},{1,17},{2,18},{3,19},{4,20},{5,21},{6,22},{7,23},{8,24},{9,... | collective-permute-start | bytes 98312 | tf_op jit(solution)/shard_map/ppermute | solution.py:497
  59.1 5.5 %collective-permute-start.24 = (f32[64,128]{1,0:T(8,128)S(1)}, f32[64,128]{1,0:T(8,128)S(1)}, u32[]{:S(2)}, u32[]{:S(2)}) collective-permute-start(f32[64,128]{1,0:T(8,128)S(1)} %get-tuple-element.135), channel_id=1, source_target_pairs={{0,25},{1,24},{2,27},{3,26},{4,29},{5,28},{6,31},{7,30},{8,17},{9,... | collective-permute-start | bytes 98312 | tf_op jit(solution)/shard_map/ppermute | solution.py:497
  68.9 14.4 %collective-permute-start.26 = (f32[192,128]{1,0:T(8,128)S(1)}, f32[192,128]{1,0:T(8,128)S(1)}, u32[]{:S(2)}, u32[]{:S(2)}) collective-permute-start(f32[192,128]{1,0:T(8,128)S(1)} %get-tuple-element.139), channel_id=1, source_target_pairs={{0,1},{1,0},{2,3},{3,2},{4,5},{5,4},{6,7},{7,6},{8,9},{9,8},{10,11... | collective-permute-start | bytes 294920 | tf_op jit(solution)/shard_map/ppermute | solution.py:497
  70.9 4.2 %collective-permute-start.29 = (f32[64,128]{1,0:T(8,128)S(1)}, f32[64,128]{1,0:T(8,128)S(1)}, u32[]{:S(2)}, u32[]{:S(2)}) collective-permute-start(f32[64,128]{1,0:T(8,128)S(1)} %get-tuple-element.143), channel_id=1, source_target_pairs={{0,7},{1,6},{2,5},{3,4},{4,3},{5,2},{6,1},{7,0},{8,15},{9,14},{10,... | collective-permute-start | bytes 98312 | tf_op jit(solution)/shard_map/ppermute | solution.py:497
  75.4 4.9 %collective-permute-start.31 = (f32[64,128]{1,0:T(8,128)S(1)}, f32[64,128]{1,0:T(8,128)S(1)}, u32[]{:S(2)}, u32[]{:S(2)}) collective-permute-start(f32[64,128]{1,0:T(8,128)S(1)} %get-tuple-element.145), channel_id=1, source_target_pairs={{0,16},{1,17},{2,18},{3,19},{4,20},{5,21},{6,22},{7,23},{8,24},{9,... | collective-permute-start | bytes 98312 | tf_op jit(solution)/shard_map/ppermute | solution.py:497
  77.9 5.5 %collective-permute-start.32 = (f32[64,128]{1,0:T(8,128)S(1)}, f32[64,128]{1,0:T(8,128)S(1)}, u32[]{:S(2)}, u32[]{:S(2)}) collective-permute-start(f32[64,128]{1,0:T(8,128)S(1)} %get-tuple-element.145), channel_id=1, source_target_pairs={{0,25},{1,24},{2,27},{3,26},{4,29},{5,28},{6,31},{7,30},{8,17},{9,... | collective-permute-start | bytes 98312 | tf_op jit(solution)/shard_map/ppermute | solution.py:497
  87.3 14.5 %collective-permute-start.34 = (f32[192,128]{1,0:T(8,128)S(1)}, f32[192,128]{1,0:T(8,128)S(1)}, u32[]{:S(2)}, u32[]{:S(2)}) collective-permute-start(f32[192,128]{1,0:T(8,128)S(1)} %get-tuple-element.149), channel_id=1, source_target_pairs={{0,1},{1,0},{2,3},{3,2},{4,5},{5,4},{6,7},{7,6},{8,9},{9,8},{10,11... | collective-permute-start | bytes 294920 | tf_op jit(solution)/shard_map/ppermute | solution.py:497
  89.4 4.2 %collective-permute-start.37 = (f32[64,128]{1,0:T(8,128)S(1)}, f32[64,128]{1,0:T(8,128)S(1)}, u32[]{:S(2)}, u32[]{:S(2)}) collective-permute-start(f32[64,128]{1,0:T(8,128)S(1)} %get-tuple-element.152), channel_id=1, source_target_pairs={{0,7},{1,6},{2,5},{3,4},{4,3},{5,2},{6,1},{7,0},{8,15},{9,14},{10,... | collective-permute-start | bytes 98312 | tf_op jit(solution)/shard_map/ppermute | solution.py:497
  93.9 4.9 %collective-permute-start.39 = (f32[64,128]{1,0:T(8,128)S(1)}, f32[64,128]{1,0:T(8,128)S(1)}, u32[]{:S(2)}, u32[]{:S(2)}) collective-permute-start(f32[64,128]{1,0:T(8,128)S(1)} %get-tuple-element.154), channel_id=1, source_target_pairs={{0,16},{1,17},{2,18},{3,19},{4,20},{5,21},{6,22},{7,23},{8,24},{9,... | collective-permute-start | bytes 98312 | tf_op jit(solution)/shard_map/ppermute | solution.py:497
  96.3 5.5 %collective-permute-start.40 = (f32[64,128]{1,0:T(8,128)S(1)}, f32[64,128]{1,0:T(8,128)S(1)}, u32[]{:S(2)}, u32[]{:S(2)}) collective-permute-start(f32[64,128]{1,0:T(8,128)S(1)} %get-tuple-element.154), channel_id=1, source_target_pairs={{0,25},{1,24},{2,27},{3,26},{4,29},{5,28},{6,31},{7,30},{8,17},{9,... | collective-permute-start | bytes 98312 | tf_op jit(solution)/shard_map/ppermute | solution.py:497
  106.0 14.4 %collective-permute-start.42 = (f32[192,128]{1,0:T(8,128)S(1)}, f32[192,128]{1,0:T(8,128)S(1)}, u32[]{:S(2)}, u32[]{:S(2)}) collective-permute-start(f32[192,128]{1,0:T(8,128)S(1)} %get-tuple-element.158), channel_id=1, source_target_pairs={{0,1},{1,0},{2,3},{3,2},{4,5},{5,4},{6,7},{7,6},{8,9},{9,8},{10,11... | collective-permute-start | bytes 294920 | tf_op jit(solution)/shard_map/ppermute | solution.py:497
  112.5 4.9 %collective-permute-start.47 = (f32[64,128]{1,0:T(8,128)S(1)}, f32[64,128]{1,0:T(8,128)S(1)}, u32[]{:S(2)}, u32[]{:S(2)}) collective-permute-start(f32[64,128]{1,0:T(8,128)S(1)} %get-tuple-element.163), channel_id=1, source_target_pairs={{0,16},{1,17},{2,18},{3,19},{4,20},{5,21},{6,22},{7,23},{8,24},{9,... | collective-permute-start | bytes 98312 | tf_op jit(solution)/shard_map/ppermute | solution.py:497
  115.0 5.5 %collective-permute-start.48 = (f32[64,128]{1,0:T(8,128)S(1)}, f32[64,128]{1,0:T(8,128)S(1)}, u32[]{:S(2)}, u32[]{:S(2)}) collective-permute-start(f32[64,128]{1,0:T(8,128)S(1)} %get-tuple-element.163), channel_id=1, source_target_pairs={{0,25},{1,24},{2,27},{3,26},{4,29},{5,28},{6,31},{7,30},{8,17},{9,... | collective-permute-start | bytes 98312 | tf_op jit(solution)/shard_map/ppermute | solution.py:497
  120.8 5.9 %collective-permute-start.51 = (f32[64,128]{1,0:T(8,128)S(1)}, f32[64,128]{1,0:T(8,128)S(1)}, u32[]{:S(2)}, u32[]{:S(2)}) collective-permute-start(f32[64,128]{1,0:T(8,128)S(1)} %get-tuple-element.170), channel_id=1, source_target_pairs={{0,5},{1,4},{2,7},{3,6},{4,1},{5,0},{6,3},{7,2},{8,13},{9,12},{10,... | collective-permute-start | bytes 98312 | tf_op jit(solution)/shard_map/ppermute | solution.py:497
  121.5 5.3 %collective-permute-start.52 = (f32[64,128]{1,0:T(8,128)S(1)}, f32[64,128]{1,0:T(8,128)S(1)}, u32[]{:S(2)}, u32[]{:S(2)}) collective-permute-start(f32[64,128]{1,0:T(8,128)S(1)} %get-tuple-element.170), channel_id=1, source_target_pairs={{0,7},{1,6},{2,5},{3,4},{4,3},{5,2},{6,1},{7,0},{8,15},{9,14},{10,... | collective-permute-start | bytes 98312 | tf_op jit(solution)/shard_map/ppermute | solution.py:497
  127.0 4.9 %collective-permute-start.55 = (f32[72,128]{1,0:T(8,128)S(1)}, f32[72,128]{1,0:T(8,128)S(1)}, u32[]{:S(2)}, u32[]{:S(2)}) collective-permute-start(f32[72,128]{1,0:T(8,128)S(1)} %get-tuple-element.173), channel_id=1, source_target_pairs={{0,16},{1,17},{2,18},{3,19},{4,20},{5,21},{6,22},{7,23},{8,24},{9,... | collective-permute-start | bytes 110600 | tf_op jit(solution)/shard_map/ppermute | solution.py:497
  129.0 5.2 %collective-permute-start.56 = (f32[72,128]{1,0:T(8,128)S(1)}, f32[72,128]{1,0:T(8,128)S(1)}, u32[]{:S(2)}, u32[]{:S(2)}) collective-permute-start(f32[72,128]{1,0:T(8,128)S(1)} %get-tuple-element.173), channel_id=1, source_target_pairs={{0,25},{1,24},{2,27},{3,26},{4,29},{5,28},{6,31},{7,30},{8,17},{9,... | collective-permute-start | bytes 110600 | tf_op jit(solution)/shard_map/ppermute | solution.py:497
  134.4 4.8 %collective-permute-start.60 = (f32[8,128]{1,0:T(8,128)S(1)}, f32[8,128]{1,0:T(8,128)S(1)}, u32[]{:S(2)}, u32[]{:S(2)}) collective-permute-start(f32[8,128]{1,0:T(8,128)S(1)} %slice_add_fusion), channel_id=1, source_target_pairs={{0,7},{1,6},{2,5},{3,4},{4,3},{5,2},{6,1},{7,0},{8,15},{9,14},{10,... | collective-permute-start | bytes 12296 | tf_op jit(solution)/shard_map/ppermute | solution.py:497
  (32 other events, 115.6 us)
